TPU v7x, 32 devices: a whole 2x2x4 slice. The times are simulated.
32 devices in a mesh: dp: 8 (over z, x), fsdp: 4 (over y, core).
Axes of the slice: x: 2, y: 2, z: 4, core: 2. Of those that a mesh axis runs over, the one named last changes fastest.
Arguments:
- text_states: bfloat16 [24, 64, 4096], P('dp', None, 'fsdp'), may hold values from -6 to 6
- cotangent: bfloat16 [24, 64, 4096], P('dp', None, 'fsdp'), may hold values from -6 to 6
- norm_gain: float32 [4096], replicated, may hold values from 0.5 to 120
- norm_bias: float32 [4096], replicated, may hold values from -3 to 3
- branch_gate: float32 [1], replicated, may hold values from 0.4 to 1.2
- query_weight: bfloat16 [4096, 16, 128], P(None, 'fsdp'), may hold values from -0.09375 to 0.09375
- latent_weight: bfloat16 [4096, 16, 256], P(None, 'fsdp'), may hold values from -0.09375 to 0.09375
- output_weight: bfloat16 [16, 128, 4096], P('fsdp'), may hold values from -0.125 to 0.125
- latents: bfloat16 [72, 64, 4096], P('dp'), may hold values from -6 to 6
- media_refs: int32 [24, 5], replicated, may hold values from -1 to 71, as said below
- media_pos: int32 [24, 64], P('dp'), may hold values from -1 to 4, as said below
- owner_map: int32 [72], replicated, may hold values from 0 to 71, as said below
Outputs:
- layer_out: bfloat16 [24, 64, 4096], P('dp', None, 'fsdp')
- out_grad: float32 [16, 128, 4096], P('fsdp', None, 'dp')
Inputs may be any that keep to these rules, and one draw needn't show every extreme that they name: `media_refs`: row s holds the ids of sequence s's images in its first 1 to 5 entries, the rest are -1; every image id stands in exactly one row. A permutation: image i's latents are storage row owner_map[i], held by data shard owner_map[i] // 9. The images of one data shard's sequences lie on at most 2 storage rows of any one data shard, and some data shard reaches 2. `media_pos`: for each token, the number of its sequence's images placed at or before it, minus one; images take increasing positions in the window, each image has tokens, and a slot named is always filled in media_refs.
All inputs are finite; a program needn't handle non-finite values.
Results may differ from a plain program's by a relative error of at most 0.039.
The roundings to bfloat16 on the way count: a program that leaves them out, or rounds other values in their place, can miss the bound.
Values may be sent and summed in bfloat16 or wider, within the bound.
No kernel may reach another device: no remote copies, remote signals or barrier semaphores. Data moves between devices by JAX's collectives and lax.ppermute only.
A program may use at most 128 MiB of HBM per device.

v0:
```python
import functools

import jax
import jax.numpy as jnp
from jax import lax
from jax.experimental import pallas as pl
from jax.experimental.pallas import tpu as pltpu
from jax.sharding import PartitionSpec as P


EPSILON = 1e-05
F32 = jnp.float32
BF16 = jnp.bfloat16


def swap(value, axis, offset):
    size = lax.axis_size(axis)
    return lax.ppermute(value, axis, [(i, i ^ offset) for i in range(size)])


def layer_norm(row_values, norm_gain, norm_bias):
    as_float = row_values.astype(F32)
    row_mean = jnp.mean(as_float, axis=-1, keepdims=True)
    centered = as_float - row_mean
    variance = jnp.mean(centered * centered, axis=-1, keepdims=True)
    return (centered * lax.rsqrt(variance + EPSILON) * norm_gain + norm_bias).astype(BF16)


def gather_blocks(value, axis):
    size = lax.axis_size(axis)
    blocks = {0: value}
    step = size // 2
    while step:
        for offset in list(blocks):
            blocks[offset | step] = swap(blocks[offset], axis, step)
        step //= 2
    return [blocks[j] for j in range(size)]


def pairs_kernel(first, heads, groups, capacity, splits, me_ref, refs_ref, owner_ref, latent_hbm, weight_hbm, *rest):
    outs, (latent_buf, weight_buf, acc, pairs, picked, sems) = rest[:groups], rest[groups:]
    images_local, latent_rows = pairs.shape[1], pairs.shape[2]
    depth = latent_hbm.shape[1] // splits
    copies = []
    for k in range(splits):
        weight_copy = pltpu.make_async_copy(weight_hbm.at[pl.ds(k * depth, depth)], weight_buf.at[k], sems.at[2 * k])
        latent_copy = pltpu.make_async_copy(latent_hbm.at[:, pl.ds(k * depth, depth)], latent_buf.at[k], sems.at[2 * k + 1])
        weight_copy.start()
        latent_copy.start()
        copies.append((weight_copy, latent_copy))

    low = me_ref[0] * images_local
    per_sequence = refs_ref.shape[0]
    sequences = refs_ref.shape[1] // groups

    def per_target(offset, carry):
        for slot in range(capacity):
            picked[offset * (capacity + 1) + slot] = 0
        count = 0
        for sequence in range(sequences):
            for position in range(per_sequence):
                image = refs_ref[position, (me_ref[0] ^ offset) * sequences + sequence]
                within = owner_ref[jnp.maximum(image, 0)] - low
                hit = (image >= 0) & (within >= 0) & (within < images_local)
                slot = jnp.where(hit, jnp.minimum(count, capacity - 1), capacity)
                picked[offset * (capacity + 1) + slot] = within
                count = count + hit.astype(jnp.int32)
        return carry

    lax.fori_loop(0, groups, per_target, 0)
    sent = []
    for k in range(splits):
        copies[k][0].wait()
        copies[k][1].wait()
        weight = jnp.swapaxes(weight_buf[k], 0, 1)
        for head in range(heads):
            part = jnp.dot(latent_buf[k], weight[first + head], preferred_element_type=F32)
            if k:
                part = acc[head] + part
            if k < splits - 1:
                acc[head] = part
                continue
            pairs[head] = part.astype(BF16).reshape(pairs.shape[1:])
            for offset in reversed(range(groups)):
                for slot in range(capacity):
                    index = picked[offset * (capacity + 1) + slot]
                    target = outs[offset].at[head, pl.ds(slot * latent_rows, latent_rows)]
                    sent.append(pltpu.make_async_copy(pairs.at[head, index], target, sems.at[2 * splits + len(sent)]))
                    sent[-1].start()
    for copy in sent:
        copy.wait()


def outgoing_pairs(me, media_refs, owner_map, latents, weight, groups, capacity, first, heads):
    images_local, latent_rows, model_width = latents.shape
    width = weight.shape[2]
    rows = images_local * latent_rows
    splits = 4
    depth = model_width // splits
    smem = pl.BlockSpec(memory_space=pltpu.SMEM)
    hbm = pl.BlockSpec(memory_space=pl.ANY)
    return pl.pallas_call(
        functools.partial(pairs_kernel, first, heads, groups, capacity, splits),
        out_shape=[jax.ShapeDtypeStruct((heads, capacity * latent_rows, width), BF16)] * groups,
        in_specs=[smem, smem, smem, hbm, hbm],
        out_specs=[hbm] * groups,
        scratch_shapes=[
            pltpu.VMEM((splits, rows, depth), BF16),
            pltpu.VMEM((splits, depth, weight.shape[1], width), BF16),
            pltpu.VMEM((heads, rows, width), F32),
            pltpu.VMEM((heads, images_local, latent_rows, width), BF16),
            pltpu.SMEM((groups * (capacity + 1),), jnp.int32),
            pltpu.SemaphoreType.DMA((2 * splits + groups * capacity * heads,)),
        ],
        cost_estimate=pl.CostEstimate(
            flops=2 * rows * model_width * heads * width, bytes_accessed=latents.size * 2 + weight.size * 2, transcendentals=0
        ),
        name="pairs",
    )(me.reshape(1), media_refs.T, owner_map, latents.reshape(rows, model_width), weight)


def attend_kernel(latent_rows, base, count, slot_ref, query_ref, *rest):
    buffers, previous, out = rest[:count], rest[count:-1], rest[-1]
    heads, per_source, width = buffers[0].shape
    head_size = width // 2
    slot = slot_ref[...] - base
    columns = lax.broadcasted_iota(jnp.int32, (slot.shape[0], count * per_source), 1) // latent_rows
    allowed = columns == slot
    here = (slot >= 0) & (slot < count * (per_source // latent_rows))
    lanes = [slice(head * head_size, (head + 1) * head_size) for head in range(heads)]
    probs = []
    for head in range(heads):
        keys = jnp.concatenate([b[head, :, :head_size] for b in buffers], axis=0)
        scores = lax.dot_general(query_ref[:, lanes[head]], keys, (((1,), (1,)), ((), ())), preferred_element_type=F32)
        scores = jnp.where(allowed, scores, -1e30)
        weights = jnp.exp(scores - jnp.max(scores, axis=-1, keepdims=True))
        probs.append((weights / jnp.sum(weights, axis=-1, keepdims=True)).astype(BF16))
    contexts = []
    for head in range(heads):
        values = jnp.concatenate([b[head, :, head_size:] for b in buffers], axis=0)
        context = jnp.dot(probs[head], values, preferred_element_type=F32).astype(BF16)
        others = previous[0][:, lanes[head]] if previous else jnp.zeros(context.shape, BF16)
        contexts.append(jnp.where(here, context, others))
    out[...] = jnp.concatenate(contexts, axis=1)


def attend(slots, queries, arrived, base, latent_rows, previous):
    heads, _, width = arrived[0].shape
    tokens = queries.shape[0]
    lanes = heads * width // 2
    wide = pl.BlockSpec((tokens, lanes), lambda i: (0, 0))
    return pl.pallas_call(
        functools.partial(attend_kernel, latent_rows, base, len(arrived)),
        grid=(1,),
        out_shape=jax.ShapeDtypeStruct((tokens, lanes), BF16),
        in_specs=[pl.BlockSpec((tokens, 1), lambda i: (0, 0)), wide]
        + [pl.BlockSpec(arrived[0].shape, lambda i: (0, 0, 0))] * len(arrived)
        + [wide] * len(previous),
        out_specs=wide,
        name="attend",
    )(slots, queries, *arrived, *previous)


def grad_kernel(members, shards, place_ref, gate_ref, *rest):
    blocks, rest = rest[:shards], rest[shards:]
    contexts, previous, out, cot = rest[: len(members)], rest[len(members) : -2], rest[-2], rest[-1]
    for i, offset in enumerate(members):
        for j in range(shards):
            cot[i, place_ref[1] ^ j] = blocks[j][place_ref[0] ^ offset]
    rows = jnp.concatenate([c[...] for c in contexts], axis=0)
    columns = cot[...].reshape(rows.shape[0], out.shape[1])
    grad = gate_ref[0] * lax.dot_general(rows, columns, (((0,), (0,)), ((), ())), preferred_element_type=F32)
    out[...] = grad + previous[0][...] if previous else grad


def grad_part(place, gate, cot_blocks, contexts, members, previous):
    count = len(contexts)
    tokens, lanes = contexts[0].shape
    groups, share, cols = cot_blocks[0].shape
    total = pl.BlockSpec((lanes, cols), lambda i: (0, 0))
    smem = pl.BlockSpec(memory_space=pltpu.SMEM)
    return pl.pallas_call(
        functools.partial(grad_kernel, members, len(cot_blocks)),
        grid=(1,),
        out_shape=jax.ShapeDtypeStruct((lanes, cols), F32),
        in_specs=[smem, smem]
        + [pl.BlockSpec((groups, share, cols), lambda i: (0, 0, 0))] * len(cot_blocks)
        + [pl.BlockSpec((tokens, lanes), lambda i: (0, 0))] * count
        + [total] * len(previous),
        out_specs=total,
        scratch_shapes=[pltpu.VMEM((count, len(cot_blocks), share, cols), BF16)],
        input_output_aliases={2 + len(cot_blocks) + count: 0} if previous else {},
        name="grad",
    )(place, gate, *cot_blocks, *contexts, *previous)


def body(
    text_states,
    cotangent,
    norm_gain,
    norm_bias,
    branch_gate,
    query_weight,
    latent_weight,
    output_weight,
    latents,
    media_refs,
    media_pos,
    owner_map,
):
    seq_local, window, feat_local = text_states.shape
    model_width = query_weight.shape[0]
    head_local, head_size = query_weight.shape[1], query_weight.shape[2]
    img_local, latent_rows = latents.shape[0], latents.shape[1]
    groups, shards = lax.axis_size("dp"), lax.axis_size("fsdp")
    me, shard = lax.axis_index("dp"), lax.axis_index("fsdp")
    per_sequence = media_refs.shape[1]
    slot_count = media_refs.shape[0] * per_sequence // groups
    capacity = (slot_count + groups - 1) // groups
    tokens = seq_local * window
    gate_scale = jnp.tanh(branch_gate)

    outgoing = outgoing_pairs(me, media_refs, owner_map, latents, latent_weight, groups, capacity, 0, head_local)
    outgoing, text_in, cotangent = lax.optimization_barrier((outgoing, text_states, cotangent))
    half = groups // 2
    arrived = {0: outgoing[0]}
    for d in range(groups - 1, 0, -1):
        arrived[d] = swap(outgoing[d], "dp", d)

    text_blocks = gather_blocks(text_in.reshape(tokens, feat_local), "fsdp")
    text_rows = jnp.zeros((tokens, model_width), BF16)
    for j, block in enumerate(text_blocks):
        text_rows = lax.dynamic_update_slice(text_rows, block, (0, (shard ^ j) * feat_local))
    normed = layer_norm(text_rows, norm_gain, norm_bias)
    queries = jnp.dot(normed, query_weight.reshape(model_width, head_local * head_size), preferred_element_type=F32)
    queries = (queries * head_size ** (-0.5)).astype(BF16)

    own_refs = lax.dynamic_slice_in_dim(media_refs, me * seq_local, seq_local, 0).reshape(slot_count)
    present = own_refs >= 0
    lookup = jnp.maximum(own_refs, 0)[:, None] == jnp.arange(owner_map.shape[0], dtype=jnp.int32)
    source = jnp.sum(jnp.where(lookup, owner_map, 0), axis=-1) // img_local
    position = jnp.arange(slot_count, dtype=jnp.int32)
    earlier = (source[:, None] == source[None, :]) & present[None, :] & (position[None, :] < position[:, None])
    slot_of = (source ^ me) * capacity + jnp.sum(earlier.astype(jnp.int32), axis=-1)
    named = media_pos[:, :, None] == jnp.arange(per_sequence, dtype=jnp.int32)
    slots = jnp.sum(jnp.where(named, slot_of.reshape(seq_local, 1, per_sequence), 0), axis=-1)
    slots = jnp.where(media_pos >= 0, slots, -1).reshape(tokens, 1)

    share = tokens // shards
    cols = model_width // groups
    cot = cotangent.reshape(tokens, feat_local)
    share_rows = jnp.zeros((shards, share, feat_local), BF16)
    for j in range(shards):
        piece = lax.dynamic_slice(cot, ((shard ^ j) * share, 0), (share, feat_local))
        piece = swap(piece, "fsdp", j) if j else piece
        share_rows = lax.dynamic_update_slice(share_rows, piece[None], (shard ^ j, 0, 0))
    share_rows = share_rows.reshape(shards, share, feat_local // cols, cols).transpose(0, 2, 1, 3)
    share_rows = lax.all_to_all(share_rows.reshape(groups, share, cols), "dp", 0, 0, tiled=True)
    cot_blocks = gather_blocks(share_rows, "fsdp")

    context = attend(slots, queries, [arrived[d] for d in range(half)], 0, latent_rows, [])
    context = attend(slots, queries, [arrived[d] for d in range(half, groups)], half * capacity, latent_rows, [context])
    gathered = {0: context}
    for d in range(groups - 2, 0, -2):
        gathered[d] = swap(context, "dp", d)
    gathered[1] = swap(context, "dp", 1)
    for d in range(2, groups, 2):
        gathered[d + 1] = swap(gathered[d], "dp", 1)

    place = jnp.stack([me, shard])
    last = max(groups - 2, groups // 2)
    out_grad = []
    for members in (range(last), range(last, groups)):
        group_contexts = [gathered[d] for d in members]
        out_grad = [grad_part(place, gate_scale, cot_blocks, group_contexts, tuple(members), out_grad)]
    out_grad = out_grad[0]
    update = jnp.dot(context, output_weight.reshape(head_local * head_size, model_width), preferred_element_type=F32)

    blocks = {
        j: lax.dynamic_slice(update, (0, (shard ^ j) * feat_local), (tokens, feat_local)) for j in range(shards)
    }
    step = 1
    while step < shards:
        kept = {}
        for j in blocks:
            if not j & step:
                received = swap(blocks[j | step].astype(BF16), "fsdp", step)
                kept[j] = blocks[j] + received.astype(F32)
        blocks = kept
        step *= 2
    layer_out = (text_states.reshape(tokens, feat_local).astype(F32) + gate_scale[0] * blocks[0]).astype(BF16)
    return (
        layer_out.reshape(seq_local, window, feat_local),
        out_grad.reshape(head_local, head_size, cols),
    )


def solution(mesh):
    in_specs = (
        P("dp", None, "fsdp"),
        P("dp", None, "fsdp"),
        P(),
        P(),
        P(),
        P(None, "fsdp", None),
        P(None, "fsdp", None),
        P("fsdp", None, None),
        P("dp", None, None),
        P(),
        P("dp", None),
        P(),
    )
    out_specs = (P("dp", None, "fsdp"), P("fsdp", None, "dp"))

    return jax.shard_map(body, mesh=mesh, in_specs=in_specs, out_specs=out_specs, check_vma=False)
```

profile of v0, /device:TPU:0, one launch (start us, length us, event | category | flops | bytes accessed | tf_op | source)
XLA Modules:
  0.0 127.3 jit_solution(13498487026290552947)
XLA Ops:
  0.7 10.2 %pairs.1 = (bf16[4,128,256]{2,1,0:T(8,128)(2,1)}, bf16[4,128,256]{2,1,0:T(8,128)(2,1)}, bf16[4,128,256]{2,1,0:T(8,128)(2,1)}, bf16[4,128,256]{2,1,0:T(8,128)(2,1...) custom-call(s32[1]{0:T(128)} %bitcast.2.me_ref, ...), custom_call_target="tpu_custom_call" | custom-call | flops 4831838208 | bytes 13107200 | tf_op jit(solution)/shard_map/pairs/pallas_call | solution.py:102
  10.9 0.6 collective-permute-start
  11.4 2.6 %collective-permute-start.1 = (bf16[192,1024]{1,0:T(8,128)(2,1)S(1)}, bf16[192,1024]{1,0:T(8,128)(2,1)S(1)}, u32[]{:S(2)}, u32[]{:S(2)}) collective-permute-start(bf16[192,1024]{1,0:T(8,128)(2,1)S(1)} %bitcast.35), channel_id=1, source_target_pairs={{0,2},{1,3},{2,0},{3,1},{4,6},{5,7},{6,4},{7,5},{8,10},{9,11},{10,... | collective-permute-start | bytes 1179656 | tf_op jit(solution)/shard_map/ppermute | solution.py:18
  14.0 2.6 %collective-permute-start.3 = (bf16[4,128,256]{2,1,0:T(8,128)(2,1)}, bf16[4,128,256]{2,1,0:T(8,128)(2,1)}, u32[]{:S(2)}, u32[]{:S(2)}) collective-permute-start(bf16[4,128,256]{2,1,0:T(8,128)(2,1)} %get-tuple-element.29), channel_id=1, source_target_pairs={{0,16},{4,20},{8,24},{12,28},{16,0},{20,4},{24,8},{28,12},{1,17},{... | collective-permute-start | bytes 786440 | tf_op jit(solution)/shard_map/ppermute | solution.py:18
  16.6 1.3 collective-permute-start.4
  17.9 0.1 collective-permute-start.13
  18.0 0.1 fusion.27
  18.1 0.1 fusion.26
  18.1 0.1 copy.21
  18.2 0.1 max.11
  18.3 0.2 select_reduce_fusion.1
  18.5 0.1 copy.22
  18.6 0.1 ge.19
  18.7 0.2 convert_reduce_fusion.1
  18.9 0.1 reduce_sum.49
  19.0 0.1 and.33
  19.1 0.1 div.28
  19.2 0.1 copy.23
  19.3 0.1 select_reduce_fusion
  19.4 0.8 reshape.135.slot_ref
  20.2 0.2 broadcast_in_dim.60
  20.5 0.6 collective-permute-start.14
  21.1 4.8 %collective-permute-done.14 = bf16[48,1024]{1,0:T(8,128)(2,1)S(1)} collective-permute-done((bf16[48,1024]{1,0:T(8,128)(2,1)S(1)}, bf16[48,1024]{1,0:T(8,128)(2,1)S(1)}, u32[]{:S(2)}, u32[]{:S(2)}) %collective-permute-start.14) | collective-permute-done | bytes 98336 | tf_op jit(solution)/shard_map/ppermute | solution.py:18
  25.8 1.0 collective-permute-start.15
  26.9 3.8 %collective-permute-done.15 = bf16[48,1024]{1,0:T(8,128)(2,1)S(1)} collective-permute-done((bf16[48,1024]{1,0:T(8,128)(2,1)S(1)}, bf16[48,1024]{1,0:T(8,128)(2,1)S(1)}, u32[]{:S(2)}, u32[]{:S(2)}) %collective-permute-start.15) | collective-permute-done | bytes 98336 | tf_op jit(solution)/shard_map/ppermute | solution.py:18
  30.6 4.0 %collective-permute-start.5 = (bf16[4,128,256]{2,1,0:T(8,128)(2,1)}, bf16[4,128,256]{2,1,0:T(8,128)(2,1)}, u32[]{:S(2)}, u32[]{:S(2)}) collective-permute-start(bf16[4,128,256]{2,1,0:T(8,128)(2,1)} %get-tuple-element.31), channel_id=1, source_target_pairs={{0,24},{4,28},{8,16},{12,20},{16,8},{20,12},{24,0},{28,4},{1,25},{... | collective-permute-start | bytes 786440 | tf_op jit(solution)/shard_map/ppermute | solution.py:18
  34.7 0.1 collective-permute-start.2
  34.8 0.8 pad_maximum_fusion
  35.6 3.8 %all-to-all-start = ((bf16[8,48,512]{2,1,0:T(8,128)(2,1)}), bf16[8,48,512]{2,1,0:T(8,128)(2,1)S(1)}, u32[]{:S(2)}, u32[]{:S(2)}) async-start(bf16[8,48,512]{2,1,0:T(8,128)(2,1)} %bitcast.14), calls=%async_computation | async-start | bytes 786432 | tf_op jit(solution)/shard_map/all_to_all | solution.py:258
  39.4 1.8 %collective-permute-start.7 = (bf16[4,128,256]{2,1,0:T(8,128)(2,1)}, bf16[4,128,256]{2,1,0:T(8,128)(2,1)S(1)}, u32[]{:S(2)}, u32[]{:S(2)}) collective-permute-start(bf16[4,128,256]{2,1,0:T(8,128)(2,1)} %get-tuple-element.34), channel_id=1, source_target_pairs={{0,4},{4,0},{8,12},{12,8},{16,20},{20,16},{24,28},{28,24},{1,5},{5... | collective-permute-start | bytes 786440 | tf_op jit(solution)/shard_map/ppermute | solution.py:18
  41.3 1.5 %collective-permute-start.8 = (bf16[4,128,256]{2,1,0:T(8,128)(2,1)}, bf16[4,128,256]{2,1,0:T(8,128)(2,1)S(1)}, u32[]{:S(2)}, u32[]{:S(2)}) collective-permute-start(bf16[4,128,256]{2,1,0:T(8,128)(2,1)} %get-tuple-element.35), channel_id=1, source_target_pairs={{0,8},{4,12},{8,0},{12,4},{16,24},{20,28},{24,16},{28,20},{1,9},{5... | collective-permute-start | bytes 786440 | tf_op jit(solution)/shard_map/ppermute | solution.py:18
  42.9 0.3 convert_reduce_fusion
  43.2 0.6 fusion.5
  43.8 11.6 %collective-permute-done.7.rest_1_ = bf16[4,128,256]{2,1,0:T(8,128)(2,1)S(1)} collective-permute-done((bf16[4,128,256]{2,1,0:T(8,128)(2,1)}, bf16[4,128,256]{2,1,0:T(8,128)(2,1)S(1)}, u32[]{:S(2)}, u32[]{:S(2)}) %collective-permute-start.7) | collective-permute-done | bytes 262176 | tf_op jit(solution)/shard_map/ppermute | solution.py:18
  55.4 3.2 %collective-permute-start.6 = (bf16[4,128,256]{2,1,0:T(8,128)(2,1)}, bf16[4,128,256]{2,1,0:T(8,128)(2,1)S(1)}, u32[]{:S(2)}, u32[]{:S(2)}) collective-permute-start(bf16[4,128,256]{2,1,0:T(8,128)(2,1)} %get-tuple-element.32), channel_id=1, source_target_pairs={{0,28},{4,24},{8,20},{12,16},{16,12},{20,8},{24,4},{28,0},{1,29},{... | collective-permute-start | bytes 786440 | tf_op jit(solution)/shard_map/ppermute | solution.py:18
  58.7 1.9 %fusion.19.query_ref = bf16[192,512]{1,0:T(8,128)(2,1)} fusion(bf16[512,8,4,128]{3,2,1,0:T(4,128)(2,1)S(1)} %bitcast.42, bf16[192,4096]{1,0:T(8,128)(2,1)S(1)} %constant_dynamic-update-slice_fusion, f32[4096]{0:T(1024)S(1)} %copy-done.19, f32[4096]{0:T(1024)S(1)} %copy-done.20, f32[192]{0:T(256)S(1)} %add_rsqrt_fusion, f32[192]{0:T(256)S(1)} %broadcast_multiply_fusion), kind=kOutput, calls=%fused_computation.16 | convolution fusion | flops 810221568 | bytes 5998080 | tf_op jit(solution)/shard_map/dot_general | solution.py:235
  60.6 13.3 %collective-permute-done.9.rest_3_ = bf16[4,128,256]{2,1,0:T(8,128)(2,1)S(1)} collective-permute-done((bf16[4,128,256]{2,1,0:T(8,128)(2,1)S(1)}, bf16[4,128,256]{2,1,0:T(8,128)(2,1)S(1)}, u32[]{:S(2)}, u32[]{:S(2)}) %collective-permute-start.9) | collective-permute-done | bytes 262176 | tf_op jit(solution)/shard_map/ppermute | solution.py:18
  74.0 0.7 copy-done.9
  74.7 3.0 %attend.2.rest_4_ = bf16[192,512]{1,0:T(8,128)(2,1)} custom-call(s32[192,1]{1,0:T(8,128)} %reshape.135.slot_ref, bf16[192,512]{1,0:T(8,128)(2,1)} %fusion.19.query_ref, bf16[4,128,256]{2,1,0:T(8,128)(2,1)} %get-tuple-element.33.rest_0_, bf16[4,128,256]{2,1,0:T(8,128)(2,1)} %copy-done.6, bf16[4,128,256]{2,1,0:T(8,128)(2,1)} %copy-done.8, ...), custom_call_target="tpu_custom_call" | custom-call | tf_op jit(solution)/shard_map/attend/pallas_call | solution.py:152
  77.7 0.7 copy-done.7
  78.4 3.0 %attend.3.rest_4_ = bf16[192,512]{1,0:T(8,128)(2,1)} custom-call(s32[192,1]{1,0:T(8,128)} %reshape.135.slot_ref, bf16[192,512]{1,0:T(8,128)(2,1)} %fusion.19.query_ref, bf16[4,128,256]{2,1,0:T(8,128)(2,1)} %collective-permute-done.3.rest_0_, bf16[4,128,256]{2,1,0:T(8,128)(2,1)} %collective-permute-done.4.rest_1_, ...), custom_call_target="tpu_custom_call" | custom-call | tf_op jit(solution)/shard_map/attend/pallas_call | solution.py:152
  81.4 3.3 %fusion.32 = f32[192,4096]{1,0:T(8,128)S(1)} fusion(bf16[192,512]{1,0:T(8,128)(2,1)} %attend.3.rest_4_, bf16[512,4096]{1,0:T(8,128)(2,1)} %bitcast.32), kind=kOutput, calls=%fused_computation.56 | convolution fusion | flops 805306368 | bytes 7536640 | tf_op jit(solution)/shard_map/dot_general | solution.py:277
  84.7 1.0 dynamic-slice_convert_fusion.1
  85.7 1.2 collective-permute-start.19
  86.9 0.5 collective-permute-start.17
  87.4 1.2 collective-permute-start.21
  88.5 2.2 %collective-permute-start.22 = (bf16[192,512]{1,0:T(8,128)(2,1)}, bf16[192,512]{1,0:T(8,128)(2,1)S(1)}, u32[]{:S(2)}, u32[]{:S(2)}) collective-permute-start(bf16[192,512]{1,0:T(8,128)(2,1)} %attend.3.rest_4_), channel_id=1, source_target_pairs={{0,8},{4,12},{8,0},{12,4},{16,24},{20,28},{24,16},{28,20},{1,9},{5... | collective-permute-start | bytes 589832 | tf_op jit(solution)/shard_map/ppermute | solution.py:18
  90.7 4.9 %collective-permute-done.19.rest_4_ = bf16[192,512]{1,0:T(8,128)(2,1)} collective-permute-done((bf16[192,512]{1,0:T(8,128)(2,1)}, bf16[192,512]{1,0:T(8,128)(2,1)}, u32[]{:S(2)}, u32[]{:S(2)}) %collective-permute-start.19) | collective-permute-done | bytes 196640 | tf_op jit(solution)/shard_map/ppermute | solution.py:18
  95.6 4.0 %collective-permute-start.24 = (bf16[192,512]{1,0:T(8,128)(2,1)}, bf16[192,512]{1,0:T(8,128)(2,1)S(1)}, u32[]{:S(2)}, u32[]{:S(2)}) collective-permute-start(bf16[192,512]{1,0:T(8,128)(2,1)} %attend.3.rest_4_), channel_id=1, source_target_pairs={{0,16},{4,20},{8,24},{12,28},{16,0},{20,4},{24,8},{28,12},{1,17},{... | collective-permute-start | bytes 589832 | tf_op jit(solution)/shard_map/ppermute | solution.py:18
  99.6 1.8 %add_convert_fusion = bf16[192,1024]{1,0:T(8,128)(2,1)} fusion(bf16[192,1024]{1,0:T(8,128)(2,1)} %collective-permute-done.11, f32[192,4096]{1,0:T(8,128)S(1)} %fusion.32, s32[]{:T(128)S(6)} %select_n.82), kind=kLoop, calls=%fused_computation.19 | loop fusion | flops 589824 | bytes 1572868 | tf_op jit(solution)/shard_map/convert_element_type | solution.py:287
  101.4 1.1 collective-permute-start.23
  102.6 0.2 collective-permute-start.18
  102.8 0.3 collective-permute-start.10
  103.1 6.1 %collective-permute-done.24.rest_8_ = bf16[192,512]{1,0:T(8,128)(2,1)S(1)} collective-permute-done((bf16[192,512]{1,0:T(8,128)(2,1)}, bf16[192,512]{1,0:T(8,128)(2,1)S(1)}, u32[]{:S(2)}, u32[]{:S(2)}) %collective-permute-start.24) | collective-permute-done | bytes 196640 | tf_op jit(solution)/shard_map/ppermute | solution.py:18
  109.2 0.5 collective-permute-start.12
  109.7 1.2 collective-permute-start.25
  110.9 0.7 copy-done.13
  111.6 0.9 collective-permute-start.20
  113.2 0.6 pad_add_fusion.place_ref
  113.8 3.7 %collective-permute-done.25.rest_9_ = bf16[192,512]{1,0:T(8,128)(2,1)S(1)} collective-permute-done((bf16[192,512]{1,0:T(8,128)(2,1)S(1)}, bf16[192,512]{1,0:T(8,128)(2,1)S(1)}, u32[]{:S(2)}, u32[]{:S(2)}) %collective-permute-start.25) | collective-permute-done | bytes 196640 | tf_op jit(solution)/shard_map/ppermute | solution.py:18
  117.5 0.7 copy-done.14
  118.2 3.6 %grad.2.rest_6_ = f32[512,512]{1,0:T(8,128)} custom-call(s32[2]{0:T(128)} %pad_add_fusion.place_ref, f32[1]{0:T(128)} %tanh.3.gate_ref, bf16[8,48,512]{2,1,0:T(8,128)(2,1)} %copy-done, bf16[8,48,512]{2,1,0:T(8,128)(2,1)} %copy-done.2, bf16[8,48,512]{2,1,0:T(8,128)(2,1)} %copy-done.1, bf16[8,48,512]{2,1,0:T(8,128)(2,1)} %collective-permute-done.18.rest_3_, ...), custom_call_target="tpu_custom_call" | custom-call | tf_op jit(solution)/shard_map/grad/pallas_call | solution.py:182
  121.8 3.3 %grad.3 = f32[512,512]{1,0:T(8,128)} custom-call(s32[2]{0:T(128)} %pad_add_fusion.place_ref, f32[1]{0:T(128)} %tanh.3.gate_ref, bf16[8,48,512]{2,1,0:T(8,128)(2,1)} %copy-done, bf16[8,48,512]{2,1,0:T(8,128)(2,1)} %copy-done.2, bf16[8,48,512]{2,1,0:T(8,128)(2,1)} %copy-done.1, ...), custom_call_target="tpu_custom_call", output_to_operand_aliasing={{}: (8, {})} | custom-call | tf_op jit(solution)/shard_map/grad/pallas_call | solution.py:182
  125.2 2.1 %fusion.24 = bf16[192,1024]{1,0:T(8,128)(2,1)} fusion(bf16[192,1024]{1,0:T(8,128)(2,1)} %collective-permute-done.12, bf16[192,1024]{1,0:T(8,128)(2,1)} %collective-permute-done.10, f32[192,4096]{1,0:T(8,128)S(1)} %fusion.32, s32[]{:T(128)S(6)} %select_n.80, bf16[3,64,1024]{2,1,0:T(8,128)(2,1)S(1)} %copy-done.4, f32[]{:T(128)} %bitcast.1), kind=kLoop, calls=%fused_computation.18 | loop fusion | flops 1572864 | bytes 2359304 | tf_op jit(solution)/shard_map/convert_element_type | solution.py:291
  (79 shorter events, 0.5 us)
Async XLA Ops:
  0.6 10.2 %copy-start.3 = (bf16[3,64,1024]{2,1,0:T(8,128)(2,1)S(1)}, bf16[3,64,1024]{2,1,0:T(8,128)(2,1)}, u32[]{:S(2)}) copy-start(bf16[3,64,1024]{2,1,0:T(8,128)(2,1)} %param.12) | copy-start | bytes 1179652
  0.6 17.2 %copy-start.5 = (bf16[3,64,1024]{2,1,0:T(8,128)(2,1)S(1)}, bf16[3,64,1024]{2,1,0:T(8,128)(2,1)}, u32[]{:S(2)}) copy-start(bf16[3,64,1024]{2,1,0:T(8,128)(2,1)} %param.13) | copy-start | bytes 1179652
  0.7 17.3 %copy-start.15 = (s32[24,5]{0,1:T(8,128)S(1)}, s32[24,5]{0,1:T(8,128)}, u32[]{:S(2)}) copy-start(s32[24,5]{0,1:T(8,128)} %param.21) | copy-start | bytes 1444
  0.7 17.6 %copy-start.21 = (s32[72]{0:T(128)S(1)}, s32[72]{0:T(128)}, u32[]{:S(2)}) copy-start(s32[72]{0:T(128)} %owner_ref.1) | copy-start | bytes 868
  0.7 18.6 %copy-start.16 = (s32[3,64]{1,0:T(4,128)S(1)}, s32[3,64]{1,0:T(4,128)}, u32[]{:S(2)}) copy-start(s32[3,64]{1,0:T(4,128)} %param.22) | copy-start | bytes 2308
  10.9 28.5 %collective-permute-start = (bf16[192,1024]{1,0:T(8,128)(2,1)S(1)}, bf16[192,1024]{1,0:T(8,128)(2,1)S(1)}, u32[]{:S(2)}, u32[]{:S(2)}) collective-permute-start(bf16[192,1024]{1,0:T(8,128)(2,1)S(1)} %bitcast.34), channel_id=1, source_target_pairs={{0,1},{1,0},{2,3},{3,2},{4,5},{5,4},{6,7},{7,6},{8,9},{9,8},{10,11... | collective-permute-start | bytes 1179656 | tf_op jit(solution)/shard_map/ppermute | solution.py:18
  11.4 23.3 %collective-permute-start.1 = (bf16[192,1024]{1,0:T(8,128)(2,1)S(1)}, bf16[192,1024]{1,0:T(8,128)(2,1)S(1)}, u32[]{:S(2)}, u32[]{:S(2)}) collective-permute-start(bf16[192,1024]{1,0:T(8,128)(2,1)S(1)} %bitcast.35), channel_id=1, source_target_pairs={{0,2},{1,3},{2,0},{3,1},{4,6},{5,7},{6,4},{7,5},{8,10},{9,11},{10,... | collective-permute-start | bytes 1179656 | tf_op jit(solution)/shard_map/ppermute | solution.py:18
  14.0 63.6 %collective-permute-start.3 = (bf16[4,128,256]{2,1,0:T(8,128)(2,1)}, bf16[4,128,256]{2,1,0:T(8,128)(2,1)}, u32[]{:S(2)}, u32[]{:S(2)}) collective-permute-start(bf16[4,128,256]{2,1,0:T(8,128)(2,1)} %get-tuple-element.29), channel_id=1, source_target_pairs={{0,16},{4,20},{8,24},{12,28},{16,0},{20,4},{24,8},{28,12},{1,17},{... | collective-permute-start | bytes 786440 | tf_op jit(solution)/shard_map/ppermute | solution.py:18
  16.6 61.0 %collective-permute-start.4 = (bf16[4,128,256]{2,1,0:T(8,128)(2,1)}, bf16[4,128,256]{2,1,0:T(8,128)(2,1)}, u32[]{:S(2)}, u32[]{:S(2)}) collective-permute-start(bf16[4,128,256]{2,1,0:T(8,128)(2,1)} %get-tuple-element.30), channel_id=1, source_target_pairs={{0,20},{4,16},{8,28},{12,24},{16,4},{20,0},{24,12},{28,8},{1,21},{... | collective-permute-start | bytes 786440 | tf_op jit(solution)/shard_map/ppermute | solution.py:18
  17.9 2.6 %collective-permute-start.13 = (bf16[48,1024]{1,0:T(8,128)(2,1)S(1)}, bf16[48,1024]{1,0:T(8,128)(2,1)S(1)}, u32[]{:S(2)}, u32[]{:S(2)}) collective-permute-start(bf16[48,1024]{1,0:T(8,128)(2,1)S(1)} %get-tuple-element.47), channel_id=1, source_target_pairs={{0,1},{1,0},{2,3},{3,2},{4,5},{5,4},{6,7},{7,6},{8,9},{9,8},{10,11... | collective-permute-start | bytes 294920 | tf_op jit(solution)/shard_map/ppermute | solution.py:18
  20.5 5.3 %collective-permute-start.14 = (bf16[48,1024]{1,0:T(8,128)(2,1)S(1)}, bf16[48,1024]{1,0:T(8,128)(2,1)S(1)}, u32[]{:S(2)}, u32[]{:S(2)}) collective-permute-start(bf16[48,1024]{1,0:T(8,128)(2,1)S(1)} %get-tuple-element.46), channel_id=1, source_target_pairs={{0,2},{1,3},{2,0},{3,1},{4,6},{5,7},{6,4},{7,5},{8,10},{9,11},{10,... | collective-permute-start | bytes 294920 | tf_op jit(solution)/shard_map/ppermute | solution.py:18
  25.8 4.8 %collective-permute-start.15 = (bf16[48,1024]{1,0:T(8,128)(2,1)S(1)}, bf16[48,1024]{1,0:T(8,128)(2,1)S(1)}, u32[]{:S(2)}, u32[]{:S(2)}) collective-permute-start(bf16[48,1024]{1,0:T(8,128)(2,1)S(1)} %get-tuple-element.45), channel_id=1, source_target_pairs={{0,3},{1,2},{2,1},{3,0},{4,7},{5,6},{6,5},{7,4},{8,11},{9,10},{10,... | collective-permute-start | bytes 294920 | tf_op jit(solution)/shard_map/ppermute | solution.py:18
  30.6 47.0 %collective-permute-start.5 = (bf16[4,128,256]{2,1,0:T(8,128)(2,1)}, bf16[4,128,256]{2,1,0:T(8,128)(2,1)}, u32[]{:S(2)}, u32[]{:S(2)}) collective-permute-start(bf16[4,128,256]{2,1,0:T(8,128)(2,1)} %get-tuple-element.31), channel_id=1, source_target_pairs={{0,24},{4,28},{8,16},{12,20},{16,8},{20,12},{24,0},{28,4},{1,25},{... | collective-permute-start | bytes 786440 | tf_op jit(solution)/shard_map/ppermute | solution.py:18
  34.7 6.6 %collective-permute-start.2 = (bf16[192,1024]{1,0:T(8,128)(2,1)S(1)}, bf16[192,1024]{1,0:T(8,128)(2,1)S(1)}, u32[]{:S(2)}, u32[]{:S(2)}) collective-permute-start(bf16[192,1024]{1,0:T(8,128)(2,1)S(1)} %collective-permute-done.1), channel_id=1, source_target_pairs={{0,1},{1,0},{2,3},{3,2},{4,5},{5,4},{6,7},{7,6},{8,9},{9,8},{10,11... | collective-permute-start | bytes 1179656 | tf_op jit(solution)/shard_map/ppermute | solution.py:18
  35.6 23.1 %copy-start.19 = (f32[4096]{0:T(1024)S(1)}, f32[4096]{0:T(1024)}, u32[]{:S(2)}) copy-start(f32[4096]{0:T(1024)} %param.15) | copy-start | bytes 49156
  35.6 51.3 %all-to-all-start = ((bf16[8,48,512]{2,1,0:T(8,128)(2,1)}), bf16[8,48,512]{2,1,0:T(8,128)(2,1)S(1)}, u32[]{:S(2)}, u32[]{:S(2)}) async-start(bf16[8,48,512]{2,1,0:T(8,128)(2,1)} %bitcast.14), calls=%async_computation | async-start | bytes 786432 | tf_op jit(solution)/shard_map/all_to_all | solution.py:258
  39.4 19.2 %copy-start.18 = (bf16[4,128,256]{2,1,0:T(8,128)(2,1)S(1)}, bf16[4,128,256]{2,1,0:T(8,128)(2,1)}, u32[]{:S(2)}) copy-start(bf16[4,128,256]{2,1,0:T(8,128)(2,1)} %get-tuple-element.36) | copy-start | bytes 786436
  39.4 19.3 %copy-start.17 = (bf16[4096,4,128]{2,1,0:T(4,128)(2,1)S(1)}, bf16[4096,4,128]{2,1,0:T(4,128)(2,1)}, u32[]{:S(2)}) copy-start(bf16[4096,4,128]{2,1,0:T(4,128)(2,1)} %param.17) | copy-start | bytes 12582916
  39.4 19.3 %copy-start.20 = (f32[4096]{0:T(1024)S(1)}, f32[4096]{0:T(1024)}, u32[]{:S(2)}) copy-start(f32[4096]{0:T(1024)} %param.14) | copy-start | bytes 49156
  39.4 15.9 %collective-permute-start.7 = (bf16[4,128,256]{2,1,0:T(8,128)(2,1)}, bf16[4,128,256]{2,1,0:T(8,128)(2,1)S(1)}, u32[]{:S(2)}, u32[]{:S(2)}) collective-permute-start(bf16[4,128,256]{2,1,0:T(8,128)(2,1)} %get-tuple-element.34), channel_id=1, source_target_pairs={{0,4},{4,0},{8,12},{12,8},{16,20},{20,16},{24,28},{28,24},{1,5},{5... | collective-permute-start | bytes 786440 | tf_op jit(solution)/shard_map/ppermute | solution.py:18
  41.3 17.3 %collective-permute-start.8 = (bf16[4,128,256]{2,1,0:T(8,128)(2,1)}, bf16[4,128,256]{2,1,0:T(8,128)(2,1)S(1)}, u32[]{:S(2)}, u32[]{:S(2)}) collective-permute-start(bf16[4,128,256]{2,1,0:T(8,128)(2,1)} %get-tuple-element.35), channel_id=1, source_target_pairs={{0,8},{4,12},{8,0},{12,4},{16,24},{20,28},{24,16},{28,20},{1,9},{5... | collective-permute-start | bytes 786440 | tf_op jit(solution)/shard_map/ppermute | solution.py:18
  55.4 5.3 %copy-start.6 = (bf16[4,128,256]{2,1,0:T(8,128)(2,1)}, bf16[4,128,256]{2,1,0:T(8,128)(2,1)S(1)}, u32[]{:S(2)}) copy-start(bf16[4,128,256]{2,1,0:T(8,128)(2,1)S(1)} %collective-permute-done.7.rest_1_) | copy-start | bytes 786436
  55.4 22.3 %collective-permute-start.6 = (bf16[4,128,256]{2,1,0:T(8,128)(2,1)}, bf16[4,128,256]{2,1,0:T(8,128)(2,1)S(1)}, u32[]{:S(2)}, u32[]{:S(2)}) collective-permute-start(bf16[4,128,256]{2,1,0:T(8,128)(2,1)} %get-tuple-element.32), channel_id=1, source_target_pairs={{0,28},{4,24},{8,20},{12,16},{16,12},{20,8},{24,4},{28,0},{1,29},{... | collective-permute-start | bytes 786440 | tf_op jit(solution)/shard_map/ppermute | solution.py:18
  58.6 2.0 %copy-start.8 = (bf16[4,128,256]{2,1,0:T(8,128)(2,1)}, bf16[4,128,256]{2,1,0:T(8,128)(2,1)S(1)}, u32[]{:S(2)}) copy-start(bf16[4,128,256]{2,1,0:T(8,128)(2,1)S(1)} %collective-permute-done.8.rest_2_) | copy-start | bytes 786436
  58.6 15.4 %collective-permute-start.9 = (bf16[4,128,256]{2,1,0:T(8,128)(2,1)S(1)}, bf16[4,128,256]{2,1,0:T(8,128)(2,1)S(1)}, u32[]{:S(2)}, u32[]{:S(2)}) collective-permute-start(bf16[4,128,256]{2,1,0:T(8,128)(2,1)S(1)} %copy-done.18), channel_id=1, source_target_pairs={{0,12},{4,8},{8,4},{12,0},{16,28},{20,24},{24,20},{28,16},{1,13},{... | collective-permute-start | bytes 786440 | tf_op jit(solution)/shard_map/ppermute | solution.py:18
  74.0 0.7 copy-start.9
  77.6 0.7 copy-start.7
  85.7 13.9 %collective-permute-start.11 = (bf16[192,1024]{1,0:T(8,128)(2,1)}, bf16[192,1024]{1,0:T(8,128)(2,1)}, u32[]{:S(2)}, u32[]{:S(2)}) collective-permute-start(bf16[192,1024]{1,0:T(8,128)(2,1)} %get-tuple-element.42), channel_id=1, source_target_pairs={{0,1},{1,0},{2,3},{3,2},{4,5},{5,4},{6,7},{7,6},{8,9},{9,8},{10,11... | collective-permute-start | bytes 1179656 | tf_op jit(solution)/shard_map/ppermute | solution.py:18
  85.7 9.9 %collective-permute-start.19 = (bf16[192,512]{1,0:T(8,128)(2,1)}, bf16[192,512]{1,0:T(8,128)(2,1)}, u32[]{:S(2)}, u32[]{:S(2)}) collective-permute-start(bf16[192,512]{1,0:T(8,128)(2,1)} %attend.3.rest_4_), channel_id=1, source_target_pairs={{0,24},{4,28},{8,16},{12,20},{16,8},{20,12},{24,0},{28,4},{1,25},{... | collective-permute-start | bytes 589832 | tf_op jit(solution)/shard_map/ppermute | solution.py:18
  86.9 31.4 %copy-start = (bf16[8,48,512]{2,1,0:T(8,128)(2,1)}, bf16[8,48,512]{2,1,0:T(8,128)(2,1)S(1)}, u32[]{:S(2)}) copy-start(bf16[8,48,512]{2,1,0:T(8,128)(2,1)S(1)} %all-to-all-done.rest_0_) | copy-start | bytes 1179652
  86.9 15.7 %collective-permute-start.17 = (bf16[8,48,512]{2,1,0:T(8,128)(2,1)S(1)}, bf16[8,48,512]{2,1,0:T(8,128)(2,1)S(1)}, u32[]{:S(2)}, u32[]{:S(2)}) collective-permute-start(bf16[8,48,512]{2,1,0:T(8,128)(2,1)S(1)} %all-to-all-done.rest_0_), channel_id=1, source_target_pairs={{0,2},{1,3},{2,0},{3,1},{4,6},{5,7},{6,4},{7,5},{8,10},{9,11},{10,... | collective-permute-start | bytes 1179656 | tf_op jit(solution)/shard_map/ppermute | solution.py:18
  87.4 15.4 %collective-permute-start.21 = (bf16[192,512]{1,0:T(8,128)(2,1)}, bf16[192,512]{1,0:T(8,128)(2,1)S(1)}, u32[]{:S(2)}, u32[]{:S(2)}) collective-permute-start(bf16[192,512]{1,0:T(8,128)(2,1)} %attend.3.rest_4_), channel_id=1, source_target_pairs={{0,4},{4,0},{8,12},{12,8},{16,20},{20,16},{24,28},{28,24},{1,5},{5... | collective-permute-start | bytes 589832 | tf_op jit(solution)/shard_map/ppermute | solution.py:18
  88.5 12.9 %collective-permute-start.22 = (bf16[192,512]{1,0:T(8,128)(2,1)}, bf16[192,512]{1,0:T(8,128)(2,1)S(1)}, u32[]{:S(2)}, u32[]{:S(2)}) collective-permute-start(bf16[192,512]{1,0:T(8,128)(2,1)} %attend.3.rest_4_), channel_id=1, source_target_pairs={{0,8},{4,12},{8,0},{12,4},{16,24},{20,28},{24,16},{28,20},{1,9},{5... | collective-permute-start | bytes 589832 | tf_op jit(solution)/shard_map/ppermute | solution.py:18
  95.6 13.6 %collective-permute-start.24 = (bf16[192,512]{1,0:T(8,128)(2,1)}, bf16[192,512]{1,0:T(8,128)(2,1)S(1)}, u32[]{:S(2)}, u32[]{:S(2)}) collective-permute-start(bf16[192,512]{1,0:T(8,128)(2,1)} %attend.3.rest_4_), channel_id=1, source_target_pairs={{0,16},{4,20},{8,24},{12,28},{16,0},{20,4},{24,8},{28,12},{1,17},{... | collective-permute-start | bytes 589832 | tf_op jit(solution)/shard_map/ppermute | solution.py:18
  99.6 10.1 %collective-permute-start.16 = (bf16[8,48,512]{2,1,0:T(8,128)(2,1)S(1)}, bf16[8,48,512]{2,1,0:T(8,128)(2,1)S(1)}, u32[]{:S(2)}, u32[]{:S(2)}) collective-permute-start(bf16[8,48,512]{2,1,0:T(8,128)(2,1)S(1)} %all-to-all-done.rest_0_), channel_id=1, source_target_pairs={{0,1},{1,0},{2,3},{3,2},{4,5},{5,4},{6,7},{7,6},{8,9},{9,8},{10,11... | collective-permute-start | bytes 1179656 | tf_op jit(solution)/shard_map/ppermute | solution.py:18
  101.4 11.1 %copy-start.11 = (bf16[192,512]{1,0:T(8,128)(2,1)}, bf16[192,512]{1,0:T(8,128)(2,1)S(1)}, u32[]{:S(2)}) copy-start(bf16[192,512]{1,0:T(8,128)(2,1)S(1)} %collective-permute-done.22.rest_6_) | copy-start | bytes 589828
  101.4 9.5 %collective-permute-start.23 = (bf16[192,512]{1,0:T(8,128)(2,1)S(1)}, bf16[192,512]{1,0:T(8,128)(2,1)S(1)}, u32[]{:S(2)}, u32[]{:S(2)}) collective-permute-start(bf16[192,512]{1,0:T(8,128)(2,1)S(1)} %collective-permute-done.22.rest_6_), channel_id=1, source_target_pairs={{0,4},{4,0},{8,12},{12,8},{16,20},{20,16},{24,28},{28,24},{1,5},{5... | collective-permute-start | bytes 589832 | tf_op jit(solution)/shard_map/ppermute | solution.py:18
  102.6 7.1 %copy-start.1 = (bf16[8,48,512]{2,1,0:T(8,128)(2,1)}, bf16[8,48,512]{2,1,0:T(8,128)(2,1)S(1)}, u32[]{:S(2)}) copy-start(bf16[8,48,512]{2,1,0:T(8,128)(2,1)S(1)} %collective-permute-done.17.rest_2_) | copy-start | bytes 1179652
  102.6 15.6 %collective-permute-start.18 = (bf16[8,48,512]{2,1,0:T(8,128)(2,1)S(1)}, bf16[8,48,512]{2,1,0:T(8,128)(2,1)}, u32[]{:S(2)}, u32[]{:S(2)}) collective-permute-start(bf16[8,48,512]{2,1,0:T(8,128)(2,1)S(1)} %collective-permute-done.17.rest_2_), channel_id=1, source_target_pairs={{0,1},{1,0},{2,3},{3,2},{4,5},{5,4},{6,7},{7,6},{8,9},{9,8},{10,11... | collective-permute-start | bytes 1179656 | tf_op jit(solution)/shard_map/ppermute | solution.py:18
  102.8 8.1 %copy-start.10 = (bf16[192,512]{1,0:T(8,128)(2,1)}, bf16[192,512]{1,0:T(8,128)(2,1)S(1)}, u32[]{:S(2)}) copy-start(bf16[192,512]{1,0:T(8,128)(2,1)S(1)} %collective-permute-done.21.rest_5_) | copy-start | bytes 589828
  102.8 22.4 %collective-permute-start.10 = (bf16[192,1024]{1,0:T(8,128)(2,1)}, bf16[192,1024]{1,0:T(8,128)(2,1)}, u32[]{:S(2)}, u32[]{:S(2)}) collective-permute-start(bf16[192,1024]{1,0:T(8,128)(2,1)} %get-tuple-element.41), channel_id=1, source_target_pairs={{0,1},{1,0},{2,3},{3,2},{4,5},{5,4},{6,7},{7,6},{8,9},{9,8},{10,11... | collective-permute-start | bytes 1179656 | tf_op jit(solution)/shard_map/ppermute | solution.py:18
  109.2 4.0 %copy-start.12 = (bf16[192,512]{1,0:T(8,128)(2,1)}, bf16[192,512]{1,0:T(8,128)(2,1)S(1)}, u32[]{:S(2)}) copy-start(bf16[192,512]{1,0:T(8,128)(2,1)S(1)} %collective-permute-done.24.rest_8_) | copy-start | bytes 589828
  109.2 16.0 %collective-permute-start.12 = (bf16[192,1024]{1,0:T(8,128)(2,1)}, bf16[192,1024]{1,0:T(8,128)(2,1)}, u32[]{:S(2)}, u32[]{:S(2)}) collective-permute-start(bf16[192,1024]{1,0:T(8,128)(2,1)} %add_convert_fusion), channel_id=1, source_target_pairs={{0,2},{1,3},{2,0},{3,1},{4,6},{5,7},{6,4},{7,5},{8,10},{9,11},{10,... | collective-permute-start | bytes 1179656 | tf_op jit(solution)/shard_map/ppermute | solution.py:18
  109.7 1.2 copy-start.2
  109.7 7.8 %collective-permute-start.25 = (bf16[192,512]{1,0:T(8,128)(2,1)S(1)}, bf16[192,512]{1,0:T(8,128)(2,1)S(1)}, u32[]{:S(2)}, u32[]{:S(2)}) collective-permute-start(bf16[192,512]{1,0:T(8,128)(2,1)S(1)} %collective-permute-done.24.rest_8_), channel_id=1, source_target_pairs={{0,4},{4,0},{8,12},{12,8},{16,20},{20,16},{24,28},{28,24},{1,5},{5... | collective-permute-start | bytes 589832 | tf_op jit(solution)/shard_map/ppermute | solution.py:18
  110.9 0.7 copy-start.13
  111.6 10.2 %collective-permute-start.20 = (bf16[192,512]{1,0:T(8,128)(2,1)}, bf16[192,512]{1,0:T(8,128)(2,1)}, u32[]{:S(2)}, u32[]{:S(2)}) collective-permute-start(bf16[192,512]{1,0:T(8,128)(2,1)} %collective-permute-done.19.rest_4_), channel_id=1, source_target_pairs={{0,4},{4,0},{8,12},{12,8},{16,20},{20,16},{24,28},{28,24},{1,5},{5... | collective-permute-start | bytes 589832 | tf_op jit(solution)/shard_map/ppermute | solution.py:18
  117.5 0.7 copy-start.14
  121.8 3.3 %copy-start.4 = (bf16[3,64,1024]{2,1,0:T(8,128)(2,1)S(1)}, bf16[3,64,1024]{2,1,0:T(8,128)(2,1)}, u32[]{:S(2)}) copy-start(bf16[3,64,1024]{2,1,0:T(8,128)(2,1)} %param.12) | copy-start | bytes 1179652
where the time goes:
time: 128 us; the launch traced here: 127 us
  waiting for transfers between devices  48.2 us (38%)
  starting transfers between devices  36.4 us (28%)
  Pallas kernels  23.1 us (18%)
  other arithmetic  6.81 us (5%)
  local copies, waits for them, and re-layouts  5.81 us (5%)
  matrix products  5.22 us (4%)
  between operations  1.73 us (1%)
    ppermute x26, waiting for transfers between devices, swap(): return lax.ppermute(value, axis, [(i, i ^ offset) for i in range(size)])  48.2 us
    ppermute x26, starting transfers between devices, swap(): return lax.ppermute(value, axis, [(i, i ^ offset) for i in range(size)])  32.7 us
    pallas_call x1, Pallas kernels, outgoing_pairs(): pl.pallas_call(functools.partial(pairs_kernel, first, heads, groups, capa...  10.2 us
    pallas_call x2, Pallas kernels, grad_part(): pl.pallas_call(functools.partial(grad_kernel, members, len(cot_blocks)),...  6.94 us
    pallas_call x2, Pallas kernels, attend(): pl.pallas_call(functools.partial(attend_kernel, latent_rows, base, len(ar...  5.97 us
    all_to_all x1, starting transfers between devices, body(): lax.all_to_all(share_rows.reshape(groups, share, cols), 'dp', 0, 0, tiled...  3.76 us
    dot_general x1, matrix products, body(): jnp.dot(context, output_weight.reshape(head_local * head_size, model_widt...  3.29 us
    unnamed x44, local copies, waits for them, and re-layouts  2.85 us
  transfers between devices with their start and end apart: 27, of which 7 were waited for; matrix products, arithmetic and copies ran while one was open for 10% of the time, Pallas kernels for 10%

commit v1 on v0

v1 whole, which is shorter than its diff:
```python
import functools

import jax
import jax.numpy as jnp
from jax import lax
from jax.experimental import pallas as pl
from jax.experimental.pallas import tpu as pltpu
from jax.sharding import PartitionSpec as P


EPSILON = 1e-05
F32 = jnp.float32
BF16 = jnp.bfloat16


VMEM = pl.BlockSpec(memory_space=pltpu.VMEM)
SMEM = pl.BlockSpec(memory_space=pltpu.SMEM)


def limit(mebibytes):
    return pltpu.CompilerParams(vmem_limit_bytes=mebibytes << 20)


def swap(value, axis, offset):
    size = lax.axis_size(axis)
    return lax.ppermute(value, axis, [(i, i ^ offset) for i in range(size)])


def norm_kernel(shards, place_ref, gain_ref, bias_ref, *rest):
    blocks, out = rest[:shards], rest[shards]
    feats = blocks[0].shape[1]
    width = shards * feats
    mean = sum(jnp.sum(block[...].astype(F32), axis=-1, keepdims=True) for block in blocks) / width
    squares = 0.0
    for block in blocks:
        centered = block[...].astype(F32) - mean
        squares = squares + jnp.sum(centered * centered, axis=-1, keepdims=True)
    scaling = lax.rsqrt(squares / width + EPSILON)
    for j, block in enumerate(blocks):
        columns = pl.ds(pl.multiple_of((place_ref[1] ^ j) * feats, 128), feats)
        centered = block[...].astype(F32) - mean
        out[:, columns] = (centered * scaling * gain_ref[:, columns] + bias_ref[:, columns]).astype(BF16)


def norm_rows(place, norm_gain, norm_bias, text_blocks):
    tokens, _ = text_blocks[0].shape
    width = norm_gain.shape[0]
    return pl.pallas_call(
        functools.partial(norm_kernel, len(text_blocks)),
        out_shape=jax.ShapeDtypeStruct((tokens, width), BF16),
        in_specs=[SMEM] + [VMEM] * (2 + len(text_blocks)),
        out_specs=VMEM,
        compiler_params=limit(12),
        name="norm",
    )(place, norm_gain.reshape(1, width), norm_bias.reshape(1, width), *text_blocks)


def gather_blocks(value, axis):
    size = lax.axis_size(axis)
    blocks = {0: value}
    step = size // 2
    while step:
        for offset in list(blocks):
            blocks[offset | step] = swap(blocks[offset], axis, step)
        step //= 2
    return [blocks[j] for j in range(size)]


def pairs_kernel(chunks, heads, groups, capacity, splits, me_ref, refs_ref, owner_ref, latent_hbm, weight_hbm, *rest):
    half = groups // 2
    outs, (latent_buf, weight_buf, acc, pairs, picked, sems) = rest[: half * chunks], rest[half * chunks :]
    images_local, latent_rows = pairs.shape[1], pairs.shape[2]
    depth = latent_hbm.shape[1] // splits
    copies = []
    for k in range(splits):
        weight_copy = pltpu.make_async_copy(weight_hbm.at[pl.ds(k * depth, depth)], weight_buf.at[k], sems.at[2 * k])
        latent_copy = pltpu.make_async_copy(latent_hbm.at[:, pl.ds(k * depth, depth)], latent_buf.at[k], sems.at[2 * k + 1])
        weight_copy.start()
        latent_copy.start()
        copies.append((weight_copy, latent_copy))

    low = me_ref[0] * images_local
    per_sequence = refs_ref.shape[0]
    sequences = refs_ref.shape[1] // groups

    def per_target(offset, carry):
        for slot in range(capacity):
            picked[offset * (capacity + 1) + slot] = 0
        count = 0
        for sequence in range(sequences):
            for position in range(per_sequence):
                image = refs_ref[position, (me_ref[0] ^ offset) * sequences + sequence]
                within = owner_ref[jnp.maximum(image, 0)] - low
                hit = (image >= 0) & (within >= 0) & (within < images_local)
                slot = jnp.where(hit, jnp.minimum(count, capacity - 1), capacity)
                picked[offset * (capacity + 1) + slot] = within
                count = count + hit.astype(jnp.int32)
        return carry

    lax.fori_loop(0, groups, per_target, 0)
    sent = []
    for k in range(splits):
        copies[k][0].wait()
        copies[k][1].wait()
        weight = jnp.swapaxes(weight_buf[k], 0, 1)
        for head in range(heads):
            part = jnp.dot(latent_buf[k], weight[head], preferred_element_type=F32)
            if k:
                part = acc[head] + part
            if k < splits - 1:
                acc[head] = part
                continue
            pairs[head] = part.astype(BF16).reshape(pairs.shape[1:])
            chunk, row = head // (heads // chunks), head % (heads // chunks)
            for offset in reversed(range(groups)):
                out = outs[chunk * half + offset % half]
                for slot in range(capacity):
                    index = picked[offset * (capacity + 1) + slot]
                    place = pl.ds((offset // half * capacity + slot) * latent_rows, latent_rows)
                    sent.append(
                        pltpu.make_async_copy(pairs.at[head, index], out.at[row, place], sems.at[2 * splits + len(sent)])
                    )
                    sent[-1].start()
    for copy in sent:
        copy.wait()


def outgoing_pairs(me, media_refs, owner_map, latents, weight, groups, capacity, chunks):
    images_local, latent_rows, model_width = latents.shape
    heads, width = weight.shape[1:]
    rows = images_local * latent_rows
    half = groups // 2
    splits = 4
    depth = model_width // splits
    hbm = pl.BlockSpec(memory_space=pl.ANY)
    shape = (heads // chunks, 2 * capacity * latent_rows, width)
    outs = pl.pallas_call(
        functools.partial(pairs_kernel, chunks, heads, groups, capacity, splits),
        out_shape=[jax.ShapeDtypeStruct(shape, BF16)] * (half * chunks),
        in_specs=[SMEM, SMEM, SMEM, hbm, hbm],
        out_specs=[hbm] * (half * chunks),
        scratch_shapes=[
            pltpu.VMEM((splits, rows, depth), BF16),
            pltpu.VMEM((splits, depth, heads, width), BF16),
            pltpu.VMEM((heads, rows, width), F32),
            pltpu.VMEM((heads, images_local, latent_rows, width), BF16),
            pltpu.SMEM((groups * (capacity + 1),), jnp.int32),
            pltpu.SemaphoreType.DMA((2 * splits + groups * capacity * heads,)),
        ],
        cost_estimate=pl.CostEstimate(
            flops=2 * rows * model_width * heads * width, bytes_accessed=latents.size * 2 + weight.size * 2, transcendentals=0
        ),
        name="pairs",
    )(me.reshape(1), media_refs.T, owner_map, latents.reshape(rows, model_width), weight)
    return [outs[chunk * half : (chunk + 1) * half] for chunk in range(chunks)]


def attend_kernel(latent_rows, chunk, count, own_slot_ref, far_slot_ref, own_query_ref, far_query_ref, *rest):
    buffers, out = rest[:count], rest[count]
    heads, both, width = buffers[0].shape
    head_size = width // 2
    per_source = both // 2
    slots = count * per_source // latent_rows
    sides = ((own_slot_ref[...], own_query_ref, 0), (far_slot_ref[...] - slots, far_query_ref, per_source))
    columns = lax.broadcasted_iota(jnp.int32, (own_slot_ref.shape[0], count * per_source), 1) // latent_rows
    lanes = [slice((chunk * heads + head) * head_size, (chunk * heads + head + 1) * head_size) for head in range(heads)]
    probs = []
    for slot, query_ref, first in sides:
        allowed = columns == slot
        for head in range(heads):
            keys = jnp.concatenate([b[head, first : first + per_source, :head_size] for b in buffers], axis=0)
            scores = lax.dot_general(
                query_ref[:, lanes[head]], keys, (((1,), (1,)), ((), ())), preferred_element_type=F32
            )
            scores = jnp.where(allowed, scores, -1e30)
            weights = jnp.exp(scores - jnp.max(scores, axis=-1, keepdims=True))
            probs.append((weights / jnp.sum(weights, axis=-1, keepdims=True)).astype(BF16))
    contexts = []
    for side, (slot, query_ref, first) in enumerate(sides):
        here = (slot >= 0) & (slot < slots)
        for head in range(heads):
            values = jnp.concatenate([b[head, first : first + per_source, head_size:] for b in buffers], axis=0)
            context = jnp.dot(probs[side * heads + head], values, preferred_element_type=F32)
            contexts.append(jnp.where(here, context, 0.0).astype(BF16))
    for side in range(2):
        out[side] = jnp.concatenate(contexts[side * heads : (side + 1) * heads], axis=1)


def attend(own_slots, far_slots, own_queries, far_queries, arrived, chunk, latent_rows):
    heads, _, width = arrived[0].shape
    return pl.pallas_call(
        functools.partial(attend_kernel, latent_rows, chunk, len(arrived)),
        out_shape=jax.ShapeDtypeStruct((2, own_queries.shape[0], heads * width // 2), BF16),
        in_specs=[VMEM] * (4 + len(arrived)),
        out_specs=VMEM,
        compiler_params=limit(12),
        name="attend",
    )(own_slots, far_slots, own_queries, far_queries, *arrived)


def join_kernel(mine_ref, other_ref, out):
    for side in range(2):
        out[side] = mine_ref[side] + other_ref[1 - side]


def join(mine, other):
    return pl.pallas_call(
        join_kernel,
        out_shape=jax.ShapeDtypeStruct(mine.shape, mine.dtype),
        in_specs=[VMEM] * 2,
        out_specs=VMEM,
        compiler_params=limit(4),
        name="join",
    )(mine, other)


def update_kernel(shards, chunks, place_ref, weight_hbm, *rest):
    contexts, outs, (weight_buf, sems) = rest[:chunks], rest[chunks : chunks + shards], rest[chunks + shards :]
    feats = outs[0].shape[1]
    copies = []
    for j in range(shards):
        columns = pl.ds(pl.multiple_of((place_ref[1] ^ j) * feats, 128), feats)
        copies.append(pltpu.make_async_copy(weight_hbm.at[:, columns], weight_buf.at[j], sems.at[j]))
    for j in reversed(range(shards)):
        copies[j].start()
    rows = jnp.concatenate([c[0] for c in contexts], axis=1)
    for j in reversed(range(shards)):
        copies[j].wait()
        outs[j][...] = jnp.dot(rows, weight_buf[j], preferred_element_type=F32).astype(BF16)


def update_terms(place, contexts, weight, shards):
    tokens, feats = contexts[0].shape[1], weight.shape[1] // shards
    return pl.pallas_call(
        functools.partial(update_kernel, shards, len(contexts)),
        in_specs=[SMEM, pl.BlockSpec(memory_space=pltpu.HBM)] + [VMEM] * len(contexts),
        out_specs=[VMEM] * shards,
        out_shape=[jax.ShapeDtypeStruct((tokens, feats), BF16)] * shards,
        scratch_shapes=[pltpu.VMEM((shards, weight.shape[0], feats), BF16), pltpu.SemaphoreType.DMA((shards,))],
        compiler_params=limit(20),
        name="update",
    )(place, weight, *contexts)


def grad_kernel(count, place_ref, gate_ref, cot_ref, *rest):
    contexts, previous, out, rows = rest[:count], rest[count:-2], rest[-2], rest[-1]
    for offset in range(count):
        for side in range(2):
            rows[place_ref[0] ^ (offset + side * count)] = contexts[offset][side]
    tokens, lanes = cot_ref.shape[0], rows.shape[2]
    grad = lax.dot_general(
        rows[...].reshape(tokens, lanes), cot_ref[...], (((0,), (0,)), ((), ())), preferred_element_type=F32
    )
    if previous:
        out[: out.shape[0] - lanes] = previous[0][...]
    out[out.shape[0] - lanes :] = gate_ref[0] * grad


def grad_part(place, gate, cot_rows, contexts, previous):
    count = len(contexts)
    _, tokens, lanes = contexts[0].shape
    rows = lanes + (previous[0].shape[0] if previous else 0)
    return pl.pallas_call(
        functools.partial(grad_kernel, count),
        out_shape=jax.ShapeDtypeStruct((rows, cot_rows.shape[1]), F32),
        in_specs=[SMEM] * 2 + [VMEM] * (1 + count + len(previous)),
        out_specs=VMEM,
        scratch_shapes=[pltpu.VMEM((2 * count, tokens, lanes), BF16)],
        compiler_params=limit(16),
        name="grad",
    )(place, gate, cot_rows, *contexts, *previous)


def body(
    text_states,
    cotangent,
    norm_gain,
    norm_bias,
    branch_gate,
    query_weight,
    latent_weight,
    output_weight,
    latents,
    media_refs,
    media_pos,
    owner_map,
):
    seq_local, window, feat_local = text_states.shape
    model_width = query_weight.shape[0]
    head_local, head_size = query_weight.shape[1], query_weight.shape[2]
    img_local, latent_rows = latents.shape[0], latents.shape[1]
    groups, shards = lax.axis_size("dp"), lax.axis_size("fsdp")
    me, shard = lax.axis_index("dp"), lax.axis_index("fsdp")
    per_sequence = media_refs.shape[1]
    slot_count = media_refs.shape[0] * per_sequence // groups
    capacity = (slot_count + groups - 1) // groups
    tokens = seq_local * window
    gate_scale = jnp.tanh(branch_gate)

    half = groups // 2
    chunks = 2 if head_local % 2 == 0 else 1
    place = jnp.stack([me, shard])

    far_pos = swap(media_pos, "dp", half)
    text_blocks = gather_blocks(text_states.reshape(tokens, feat_local), "fsdp")
    outgoing = outgoing_pairs(me, media_refs, owner_map, latents, latent_weight, groups, capacity, chunks)
    arrived = []
    for chunk in range(chunks):
        received = {o: swap(outgoing[chunk][o], "dp", o) for o in range(half - 1, 0, -1)}
        arrived.append([outgoing[chunk][0]] + [received[o] for o in range(1, half)])

    normed = norm_rows(place, norm_gain, norm_bias, text_blocks)
    queries = jnp.dot(normed, query_weight.reshape(model_width, head_local * head_size), preferred_element_type=F32)
    queries = (queries * head_size ** (-0.5)).astype(BF16)
    far_queries = swap(queries, "dp", half)

    tables = (queries, media_pos, far_pos, media_refs, owner_map)
    queries, media_pos, far_pos, media_refs, owner_map = lax.optimization_barrier(tables)

    def slots_of(group, positions):
        refs = lax.dynamic_slice_in_dim(media_refs, group * seq_local, seq_local, 0).reshape(slot_count)
        present = refs >= 0
        lookup = jnp.maximum(refs, 0)[:, None] == jnp.arange(owner_map.shape[0], dtype=jnp.int32)
        source = jnp.sum(jnp.where(lookup, owner_map, 0), axis=-1) // img_local
        position = jnp.arange(slot_count, dtype=jnp.int32)
        earlier = (source[:, None] == source[None, :]) & present[None, :] & (position[None, :] < position[:, None])
        slot_of = (source ^ group) * capacity + jnp.sum(earlier.astype(jnp.int32), axis=-1)
        named = positions[:, :, None] == jnp.arange(per_sequence, dtype=jnp.int32)
        slots = jnp.sum(jnp.where(named, slot_of.reshape(seq_local, 1, per_sequence), 0), axis=-1)
        return jnp.where(positions >= 0, slots, -1).reshape(tokens, 1)

    own_slots = slots_of(me, media_pos)
    far_slots = slots_of(me ^ half, far_pos)

    share = tokens // shards
    cols = model_width // groups
    cot = cotangent.reshape(tokens, feat_local)
    pieces = []
    for j in range(shards):
        piece = lax.dynamic_slice(cot, ((shard ^ j) * share, 0), (share, feat_local))
        pieces.append(swap(piece, "fsdp", j) if j else piece)
    pieces, queries = lax.optimization_barrier((pieces, queries))
    share_rows = jnp.zeros((shards, share, feat_local), BF16)
    for j in range(shards):
        share_rows = lax.dynamic_update_slice(share_rows, pieces[j][None], (shard ^ j, 0, 0))
    share_rows = share_rows.reshape(shards, share, feat_local // cols, cols).transpose(0, 2, 1, 3)
    share_rows = lax.all_to_all(share_rows.reshape(groups, share, cols), "dp", 0, 0, tiled=True)
    cot_blocks = gather_blocks(share_rows, "fsdp")
    cot_rows = jnp.zeros((groups, shards, share, cols), BF16)
    for j, block in enumerate(cot_blocks):
        cot_rows = lax.dynamic_update_slice(cot_rows, block[:, None], (0, shard ^ j, 0, 0))
    cot_rows = cot_rows.reshape(groups * tokens, cols)

    contexts, out_grad = [], []
    for chunk in range(chunks):
        partial = attend(own_slots, far_slots, queries, far_queries, arrived[chunk], chunk, latent_rows)
        other = swap(partial, "dp", half)
        context = join(partial, other)
        contexts.append(context)
        gathered = {0: context}
        for o in range(half - 2, 0, -2):
            gathered[o] = swap(context, "dp", o)
        gathered[1] = swap(context, "dp", 1)
        for o in range(half - 2, 0, -2):
            gathered[o + 1] = swap(gathered[o], "dp", 1)
        group_contexts = [gathered[o] for o in range(half)]
        out_grad = [grad_part(place, gate_scale, cot_rows, group_contexts, out_grad)]
    out_grad = out_grad[0]

    weight_rows = output_weight.reshape(head_local * head_size, model_width)
    blocks = dict(enumerate(update_terms(place, contexts, weight_rows, shards)))
    step = 1
    while step < shards:
        kept = {}
        for j in blocks:
            if not j & step:
                received = swap(blocks[j | step].astype(BF16), "fsdp", step)
                kept[j] = blocks[j].astype(F32) + received.astype(F32)
        blocks = kept
        step *= 2
    layer_out = (text_states.reshape(tokens, feat_local).astype(F32) + gate_scale[0] * blocks[0]).astype(BF16)
    return (
        layer_out.reshape(seq_local, window, feat_local),
        out_grad.reshape(head_local, head_size, cols),
    )


def solution(mesh):
    in_specs = (
        P("dp", None, "fsdp"),
        P("dp", None, "fsdp"),
        P(),
        P(),
        P(),
        P(None, "fsdp", None),
        P(None, "fsdp", None),
        P("fsdp", None, None),
        P("dp", None, None),
        P(),
        P("dp", None),
        P(),
    )
    out_specs = (P("dp", None, "fsdp"), P("fsdp", None, "dp"))

    return jax.shard_map(body, mesh=mesh, in_specs=in_specs, out_specs=out_specs, check_vma=False)
```

time: 128 us -> 125 us (0.977)
  waiting for transfers between devices: 48.2 us -> 55.2 us
  other arithmetic: 6.81 us -> 3.96 us
  local copies, waits for them, and re-layouts: 5.81 us -> 3.24 us
  Pallas kernels: 23.1 us -> 20.6 us
  matrix products: 5.22 us -> 3.26 us
    ppermute x26 -> x28, waiting for transfers between devices: 48.2 us -> 55.2 us  [swap(): return lax.ppermute(value, axis, [(i, i ^ offset) for i in range(size)])]
    dot_general x1 -> x0, matrix products: 3.29 us -> none  [body(): jnp.dot(context, output_weight.reshape(head_local * head_size, model_widt...]
    unnamed x44 -> x20, local copies, waits for them, and re-layouts: 2.85 us -> 0.05 us
    pallas_call x5 -> x9, Pallas kernels: 23.1 us -> 20.6 us  [the longest x1 10.2 us: outgoing_pairs(): pl.pallas_call(functools.partial(pairs_kernel, chunks, heads, groups, cap...]
    dot_general x1, matrix products: 1.92 us -> 3.26 us  [body(): jnp.dot(normed, query_weight.reshape(model_width, head_local * head_size)...]
    ppermute x26 -> x28, starting transfers between devices: 32.7 us -> 33.2 us  [swap(): return lax.ppermute(value, axis, [(i, i ^ offset) for i in range(size)])]
  transfers between devices with their start and end apart: 27 -> 29, of which waited for: 7 -> 8; matrix products, arithmetic and copies ran while one was open for 10% -> 8% of each run, Pallas kernels for 10% -> 15%
where the time goes in v1:
time: 125 us
  waiting for transfers between devices  55.2 us (44%)
  starting transfers between devices  36.9 us (30%)
  Pallas kernels  20.6 us (16%)
  other arithmetic  3.96 us (3%)
  matrix products  3.26 us (3%)
  local copies, waits for them, and re-layouts  3.24 us (3%)
  between operations  1.72 us (1%)
    ppermute x28, waiting for transfers between devices, swap(): return lax.ppermute(value, axis, [(i, i ^ offset) for i in range(size)])  55.2 us
    ppermute x28, starting transfers between devices, swap(): return lax.ppermute(value, axis, [(i, i ^ offset) for i in range(size)])  33.2 us
    pallas_call x1, Pallas kernels, outgoing_pairs(): pl.pallas_call(functools.partial(pairs_kernel, chunks, heads, groups, cap...  10.2 us
    all_to_all x1, starting transfers between devices, body(): lax.all_to_all(share_rows.reshape(groups, share, cols), 'dp', 0, 0, tiled...  3.77 us
    pallas_call x2, Pallas kernels, grad_part(): pl.pallas_call(functools.partial(grad_kernel, count), out_shape=jax.Shape...  3.36 us
    dot_general x1, matrix products, body(): jnp.dot(normed, query_weight.reshape(model_width, head_local * head_size)...  3.26 us
    pallas_call x1, Pallas kernels, update_terms(): pl.pallas_call(functools.partial(update_kernel, shards, len(contexts)), i...  2.9 us
  transfers between devices with their start and end apart: 29, of which 8 were waited for; matrix products, arithmetic and copies ran while one was open for 8% of the time, Pallas kernels for 15%

profile of v1, /device:TPU:0, one launch (start us, length us, event | category | flops | bytes accessed | tf_op | source)
XLA Modules:
  0.0 124.9 jit_solution(7660169873086391237)
XLA Ops:
  0.6 3.1 %collective-permute-start.1 = (bf16[192,1024]{1,0:T(8,128)(2,1)}, bf16[192,1024]{1,0:T(8,128)(2,1)S(1)}, u32[]{:S(2)}, u32[]{:S(2)}) collective-permute-start(bf16[192,1024]{1,0:T(8,128)(2,1)} %bitcast.49), channel_id=1, source_target_pairs={{0,2},{1,3},{2,0},{3,1},{4,6},{5,7},{6,4},{7,5},{8,10},{9,11},{10,... | collective-permute-start | bytes 1179656 | tf_op jit(solution)/shard_map/ppermute | solution.py:26
  3.7 1.1 constant_dynamic-slice_fusion
  4.8 0.6 collective-permute-start.4
  5.4 1.3 %collective-permute-start.6 = (bf16[48,1024]{1,0:T(8,128)(2,1)S(1)}, bf16[48,1024]{1,0:T(8,128)(2,1)S(1)}, u32[]{:S(2)}, u32[]{:S(2)}) collective-permute-start(bf16[48,1024]{1,0:T(8,128)(2,1)S(1)} %get-tuple-element.56), channel_id=1, source_target_pairs={{0,3},{1,2},{2,1},{3,0},{4,7},{5,6},{6,5},{7,4},{8,11},{9,10},{10,... | collective-permute-start | bytes 294920 | tf_op jit(solution)/shard_map/ppermute | solution.py:26
  6.8 7.0 %collective-permute-done.1.rest_2_ = bf16[192,1024]{1,0:T(8,128)(2,1)S(1)} collective-permute-done((bf16[192,1024]{1,0:T(8,128)(2,1)}, bf16[192,1024]{1,0:T(8,128)(2,1)S(1)}, u32[]{:S(2)}, u32[]{:S(2)}) %collective-permute-start.1) | collective-permute-done | bytes 393248 | tf_op jit(solution)/shard_map/ppermute | solution.py:26
  13.9 10.2 %pairs.1 = (bf16[2,256,256]{2,1,0:T(8,128)(2,1)}, bf16[2,256,256]{2,1,0:T(8,128)(2,1)}, bf16[2,256,256]{2,1,0:T(8,128)(2,1)}, bf16[2,256,256]{2,1,0:T(8,128)(2,1...) custom-call(s32[1]{0:T(128)} %bitcast.2.me_ref, ...), custom_call_target="tpu_custom_call" | custom-call | flops 4831838208 | bytes 13107200 | tf_op jit(solution)/shard_map/pairs/pallas_call | solution.py:137
  24.1 3.2 %collective-permute-start.3 = (s32[3,64]{1,0:T(4,128)S(1)}, s32[3,64]{1,0:T(4,128)S(1)}, u32[]{:S(2)}, u32[]{:S(2)}) collective-permute-start(s32[3,64]{1,0:T(4,128)S(1)} %copy-done.7), channel_id=1, source_target_pairs={{0,16},{4,20},{8,24},{12,28},{16,0},{20,4},{24,8},{28,12},{1,17},{... | collective-permute-start | bytes 2312 | tf_op jit(solution)/shard_map/ppermute | solution.py:26
  27.2 2.5 %collective-permute-start.10 = (bf16[2,256,256]{2,1,0:T(8,128)(2,1)}, bf16[2,256,256]{2,1,0:T(8,128)(2,1)S(1)}, u32[]{:S(2)}, u32[]{:S(2)}) collective-permute-start(bf16[2,256,256]{2,1,0:T(8,128)(2,1)} %get-tuple-element.33), channel_id=1, source_target_pairs={{0,12},{4,8},{8,4},{12,0},{16,28},{20,24},{24,20},{28,16},{1,13},{... | collective-permute-start | bytes 786440 | tf_op jit(solution)/shard_map/ppermute | solution.py:26
  29.8 2.1 %norm.1 = bf16[192,4096]{1,0:T(8,128)(2,1)S(1)} custom-call(s32[2]{0:T(128)S(1)} %pad_add_fusion.place_ref, f32[1,4096]{1,0:T(1,128)S(1)} %bitcast.52, f32[1,4096]{1,0:T(1,128)S(1)} %bitcast.53, bf16[192,1024]{1,0:T(8,128)(2,1)S(1)} %bitcast.51, bf16[192,1024]{1,0:T(8,128)(2,1)S(1)} %collective-permute-done.rest_1_, ...), custom_call_target="tpu_custom_call" | custom-call | tf_op jit(solution)/shard_map/norm/pallas_call | solution.py:48
  31.9 3.3 %fusion.6.own_query_ref = bf16[192,512]{1,0:T(8,128)(2,1)S(1)} fusion(bf16[192,4096]{1,0:T(8,128)(2,1)S(1)} %norm.1, bf16[512,8,4,128]{3,2,1,0:T(4,128)(2,1)} %bitcast.59), kind=kOutput, calls=%fused_computation.4 | convolution fusion | flops 805502976 | bytes 5963776 | tf_op jit(solution)/shard_map/dot_general | solution.py:313
  35.2 0.6 collective-permute-start.8
  36.0 0.5 collective-permute-start.9
  36.5 1.5 %collective-permute-start.12 = (bf16[2,256,256]{2,1,0:T(8,128)(2,1)}, bf16[2,256,256]{2,1,0:T(8,128)(2,1)S(1)}, u32[]{:S(2)}, u32[]{:S(2)}) collective-permute-start(bf16[2,256,256]{2,1,0:T(8,128)(2,1)} %get-tuple-element.35), channel_id=1, source_target_pairs={{0,4},{4,0},{8,12},{12,8},{16,20},{20,16},{24,28},{28,24},{1,5},{5... | collective-permute-start | bytes 786440 | tf_op jit(solution)/shard_map/ppermute | solution.py:26
  38.0 1.6 %collective-permute-start.13 = (bf16[2,256,256]{2,1,0:T(8,128)(2,1)}, bf16[2,256,256]{2,1,0:T(8,128)(2,1)S(1)}, u32[]{:S(2)}, u32[]{:S(2)}) collective-permute-start(bf16[2,256,256]{2,1,0:T(8,128)(2,1)} %get-tuple-element.36), channel_id=1, source_target_pairs={{0,8},{4,12},{8,0},{12,4},{16,24},{20,28},{24,16},{28,20},{1,9},{5... | collective-permute-start | bytes 786440 | tf_op jit(solution)/shard_map/ppermute | solution.py:26
  39.7 0.8 pad_maximum_fusion
  40.5 3.8 %all-to-all-start = ((bf16[8,48,512]{2,1,0:T(8,128)(2,1)}), bf16[8,48,512]{2,1,0:T(8,128)(2,1)S(1)}, u32[]{:S(2)}, u32[]{:S(2)}) async-start(bf16[8,48,512]{2,1,0:T(8,128)(2,1)} %bitcast.15), calls=%async_computation | async-start | bytes 786432 | tf_op jit(solution)/shard_map/all_to_all | solution.py:347
  44.3 0.1 copy.32
  44.4 0.1 max.21
  44.5 0.1 copy.35
  44.5 0.1 max.23
  44.6 0.2 select_reduce_fusion.2
  44.8 0.1 copy.33
  44.9 0.1 ge.28
  45.0 0.2 convert_reduce_fusion.1
  45.2 0.1 reduce_sum.60
  45.3 0.1 div.41
  45.4 0.1 and.62
  45.5 0.1 copy.36
  45.6 0.1 ge.31
  45.7 0.2 convert_reduce_fusion
  45.9 0.1 reduce_sum.64
  46.1 0.1 and.67
  46.2 0.1 copy.34
  46.3 0.1 select_reduce_fusion.1
  46.3 0.1 copy.37
  46.4 2.7 %collective-permute-start.14 = (bf16[2,256,256]{2,1,0:T(8,128)(2,1)}, bf16[2,256,256]{2,1,0:T(8,128)(2,1)S(1)}, u32[]{:S(2)}, u32[]{:S(2)}) collective-permute-start(bf16[2,256,256]{2,1,0:T(8,128)(2,1)} %get-tuple-element.37), channel_id=1, source_target_pairs={{0,12},{4,8},{8,4},{12,0},{16,28},{20,24},{24,20},{28,16},{1,13},{... | collective-permute-start | bytes 786440 | tf_op jit(solution)/shard_map/ppermute | solution.py:26
  49.2 2.5 %collective-permute-start.7 = (bf16[192,512]{1,0:T(8,128)(2,1)S(1)}, bf16[192,512]{1,0:T(8,128)(2,1)S(1)}, u32[]{:S(2)}, u32[]{:S(2)}) collective-permute-start(bf16[192,512]{1,0:T(8,128)(2,1)S(1)} %fusion.6.own_query_ref), channel_id=1, source_target_pairs={{0,16},{4,20},{8,24},{12,28},{16,0},{20,4},{24,8},{28,12},{1,17},{... | collective-permute-start | bytes 589832 | tf_op jit(solution)/shard_map/ppermute | solution.py:26
  51.6 0.1 reshape.203.own_slot_ref
  51.8 0.1 reshape.204.far_slot_ref
  51.9 11.9 %collective-permute-done.7.far_query_ref = bf16[192,512]{1,0:T(8,128)(2,1)S(1)} collective-permute-done((bf16[192,512]{1,0:T(8,128)(2,1)S(1)}, bf16[192,512]{1,0:T(8,128)(2,1)S(1)}, u32[]{:S(2)}, u32[]{:S(2)}) %collective-permute-start.7) | collective-permute-done | bytes 196640 | tf_op jit(solution)/shard_map/ppermute | solution.py:26
  63.9 1.0 attend.2.mine_ref
  64.9 3.4 %collective-permute-start.11 = (bf16[2,192,256]{2,1,0:T(8,128)(2,1)S(1)}, bf16[2,192,256]{2,1,0:T(8,128)(2,1)S(1)}, u32[]{:S(2)}, u32[]{:S(2)}) collective-permute-start(bf16[2,192,256]{2,1,0:T(8,128)(2,1)S(1)} %attend.2.mine_ref), channel_id=1, source_target_pairs={{0,16},{4,20},{8,24},{12,28},{16,0},{20,4},{24,8},{28,12},{1,17},{... | collective-permute-start | bytes 589832 | tf_op jit(solution)/shard_map/ppermute | solution.py:26
  68.3 1.0 attend.3.mine_ref
  69.4 0.1 collective-permute-start.15
  69.5 12.3 %collective-permute-done.11.other_ref = bf16[2,192,256]{2,1,0:T(8,128)(2,1)S(1)} collective-permute-done((bf16[2,192,256]{2,1,0:T(8,128)(2,1)S(1)}, bf16[2,192,256]{2,1,0:T(8,128)(2,1)S(1)}, u32[]{:S(2)}, u32[]{:S(2)}) %collective-permute-start.11) | collective-permute-done | bytes 196640 | tf_op jit(solution)/shard_map/ppermute | solution.py:26
  81.8 3.0 %collective-permute-done.15.other_ref = bf16[2,192,256]{2,1,0:T(8,128)(2,1)S(1)} collective-permute-done((bf16[2,192,256]{2,1,0:T(8,128)(2,1)S(1)}, bf16[2,192,256]{2,1,0:T(8,128)(2,1)S(1)}, u32[]{:S(2)}, u32[]{:S(2)}) %collective-permute-start.15) | collective-permute-done | bytes 196640 | tf_op jit(solution)/shard_map/ppermute | solution.py:26
  84.9 2.9 %update.1 = (bf16[192,1024]{1,0:T(8,128)(2,1)S(1)}, bf16[192,1024]{1,0:T(8,128)(2,1)S(1)}, bf16[192,1024]{1,0:T(8,128)(2,1)S(1)}, bf16[192,1024]{1,0:T(8,128)(2,1)S(1)}) custom-call(s32[2]{0:T(128)S(1)} %pad_add_fusion.place_ref, bf16[512,4096]{1,0:T(8,128)(2,1)S(1)} %bitcast.48, bf16[2,192,256]{2,1,0:T(8,128)(2,1)S(1)} %join.2.rest_0_, ...), custom_call_target="tpu_custom_call" | custom-call | tf_op jit(solution)/shard_map/update/pallas_call | solution.py:234
  88.6 2.0 %collective-permute-start.23 = (bf16[2,192,256]{2,1,0:T(8,128)(2,1)S(1)}, bf16[2,192,256]{2,1,0:T(8,128)(2,1)S(1)}, u32[]{:S(2)}, u32[]{:S(2)}) collective-permute-start(bf16[2,192,256]{2,1,0:T(8,128)(2,1)S(1)} %join.3.rest_1_.rest_0_), channel_id=1, source_target_pairs={{0,8},{4,12},{8,0},{12,4},{16,24},{20,28},{24,16},{28,20},{1,9},{5... | collective-permute-start | bytes 589832 | tf_op jit(solution)/shard_map/ppermute | solution.py:26
  90.6 1.5 %collective-permute-start.20 = (bf16[8,48,512]{2,1,0:T(8,128)(2,1)S(1)}, bf16[8,48,512]{2,1,0:T(8,128)(2,1)S(1)}, u32[]{:S(2)}, u32[]{:S(2)}) collective-permute-start(bf16[8,48,512]{2,1,0:T(8,128)(2,1)S(1)} %all-to-all-done), channel_id=1, source_target_pairs={{0,2},{1,3},{2,0},{3,1},{4,6},{5,7},{6,4},{7,5},{8,10},{9,11},{10,... | collective-permute-start | bytes 1179656 | tf_op jit(solution)/shard_map/ppermute | solution.py:26
  92.2 0.2 broadcast_in_dim.87
  92.4 0.3 collective-permute-start.16
  92.7 1.1 add_convert_fusion.1
  93.8 0.6 collective-permute-start.18
  94.4 8.2 %collective-permute-done.20 = bf16[8,48,512]{2,1,0:T(8,128)(2,1)S(1)} collective-permute-done((bf16[8,48,512]{2,1,0:T(8,128)(2,1)S(1)}, bf16[8,48,512]{2,1,0:T(8,128)(2,1)S(1)}, u32[]{:S(2)}, u32[]{:S(2)}) %collective-permute-start.20) | collective-permute-done | bytes 393248 | tf_op jit(solution)/shard_map/ppermute | solution.py:26
  102.7 1.6 %collective-permute-start.25 = (bf16[2,192,256]{2,1,0:T(8,128)(2,1)S(1)}, bf16[2,192,256]{2,1,0:T(8,128)(2,1)S(1)}, u32[]{:S(2)}, u32[]{:S(2)}) collective-permute-start(bf16[2,192,256]{2,1,0:T(8,128)(2,1)S(1)} %join.2.rest_0_), channel_id=1, source_target_pairs={{0,4},{4,0},{8,12},{12,8},{16,20},{20,16},{24,28},{28,24},{1,5},{5... | collective-permute-start | bytes 589832 | tf_op jit(solution)/shard_map/ppermute | solution.py:26
  104.3 0.5 collective-permute-start.22
  104.8 1.5 %collective-permute-start.27 = (bf16[2,192,256]{2,1,0:T(8,128)(2,1)S(1)}, bf16[2,192,256]{2,1,0:T(8,128)(2,1)S(1)}, u32[]{:S(2)}, u32[]{:S(2)}) collective-permute-start(bf16[2,192,256]{2,1,0:T(8,128)(2,1)S(1)} %collective-permute-done.26.rest_2_), channel_id=1, source_target_pairs={{0,4},{4,0},{8,12},{12,8},{16,20},{20,16},{24,28},{28,24},{1,5},{5... | collective-permute-start | bytes 589832 | tf_op jit(solution)/shard_map/ppermute | solution.py:26
  106.3 4.3 %collective-permute-done.18 = bf16[192,1024]{1,0:T(8,128)(2,1)S(1)} collective-permute-done((bf16[192,1024]{1,0:T(8,128)(2,1)S(1)}, bf16[192,1024]{1,0:T(8,128)(2,1)S(1)}, u32[]{:S(2)}, u32[]{:S(2)}) %collective-permute-start.18) | collective-permute-done | bytes 393248 | tf_op jit(solution)/shard_map/ppermute | solution.py:26
  110.6 1.5 %collective-permute-start.24 = (bf16[2,192,256]{2,1,0:T(8,128)(2,1)S(1)}, bf16[2,192,256]{2,1,0:T(8,128)(2,1)S(1)}, u32[]{:S(2)}, u32[]{:S(2)}) collective-permute-start(bf16[2,192,256]{2,1,0:T(8,128)(2,1)S(1)} %collective-permute-done.23.rest_2_), channel_id=1, source_target_pairs={{0,4},{4,0},{8,12},{12,8},{16,20},{20,16},{24,28},{28,24},{1,5},{5... | collective-permute-start | bytes 589832 | tf_op jit(solution)/shard_map/ppermute | solution.py:26
  112.1 1.1 add_convert_fusion
  113.2 5.8 %collective-permute-done.27.rest_3_ = bf16[2,192,256]{2,1,0:T(8,128)(2,1)S(1)} collective-permute-done((bf16[2,192,256]{2,1,0:T(8,128)(2,1)S(1)}, bf16[2,192,256]{2,1,0:T(8,128)(2,1)S(1)}, u32[]{:S(2)}, u32[]{:S(2)}) %collective-permute-start.27) | collective-permute-done | bytes 196640 | tf_op jit(solution)/shard_map/ppermute | solution.py:26
  119.0 1.2 grad.2.rest_4_
  120.2 2.5 %collective-permute-done.24.rest_3_ = bf16[2,192,256]{2,1,0:T(8,128)(2,1)S(1)} collective-permute-done((bf16[2,192,256]{2,1,0:T(8,128)(2,1)S(1)}, bf16[2,192,256]{2,1,0:T(8,128)(2,1)S(1)}, u32[]{:S(2)}, u32[]{:S(2)}) %collective-permute-start.24) | collective-permute-done | bytes 196640 | tf_op jit(solution)/shard_map/ppermute | solution.py:26
  122.7 2.2 %grad.3 = f32[512,512]{1,0:T(8,128)} custom-call(s32[2]{0:T(128)S(1)} %pad_add_fusion.place_ref, f32[1]{0:T(128)} %tanh.3.gate_ref, bf16[1536,512]{1,0:T(8,128)(2,1)S(1)} %bitcast.47, bf16[2,192,256]{2,1,0:T(8,128)(2,1)S(1)} %join.3.rest_1_.rest_0_, bf16[2,192,256]{2,1,0:T(8,128)(2,1)S(1)} %collective-permute-done.22.rest_1_, ...), custom_call_target="tpu_custom_call" | custom-call | tf_op jit(solution)/shard_map/grad/pallas_call | solution.py:263
  (70 shorter events, 1.1 us)
Async XLA Ops:
  0.6 13.2 %collective-permute-start.1 = (bf16[192,1024]{1,0:T(8,128)(2,1)}, bf16[192,1024]{1,0:T(8,128)(2,1)S(1)}, u32[]{:S(2)}, u32[]{:S(2)}) collective-permute-start(bf16[192,1024]{1,0:T(8,128)(2,1)} %bitcast.49), channel_id=1, source_target_pairs={{0,2},{1,3},{2,0},{3,1},{4,6},{5,7},{6,4},{7,5},{8,10},{9,11},{10,... | collective-permute-start | bytes 1179656 | tf_op jit(solution)/shard_map/ppermute | solution.py:26
  3.7 20.4 %collective-permute-start = (bf16[192,1024]{1,0:T(8,128)(2,1)}, bf16[192,1024]{1,0:T(8,128)(2,1)S(1)}, u32[]{:S(2)}, u32[]{:S(2)}) collective-permute-start(bf16[192,1024]{1,0:T(8,128)(2,1)} %bitcast.50), channel_id=1, source_target_pairs={{0,1},{1,0},{2,3},{3,2},{4,5},{5,4},{6,7},{7,6},{8,9},{9,8},{10,11... | collective-permute-start | bytes 1179656 | tf_op jit(solution)/shard_map/ppermute | solution.py:26
  4.8 31.2 %collective-permute-start.4 = (bf16[48,1024]{1,0:T(8,128)(2,1)S(1)}, bf16[48,1024]{1,0:T(8,128)(2,1)S(1)}, u32[]{:S(2)}, u32[]{:S(2)}) collective-permute-start(bf16[48,1024]{1,0:T(8,128)(2,1)S(1)} %get-tuple-element.58), channel_id=1, source_target_pairs={{0,1},{1,0},{2,3},{3,2},{4,5},{5,4},{6,7},{7,6},{8,9},{9,8},{10,11... | collective-permute-start | bytes 294920 | tf_op jit(solution)/shard_map/ppermute | solution.py:26
  5.3 31.1 %collective-permute-start.5 = (bf16[48,1024]{1,0:T(8,128)(2,1)S(1)}, bf16[48,1024]{1,0:T(8,128)(2,1)S(1)}, u32[]{:S(2)}, u32[]{:S(2)}) collective-permute-start(bf16[48,1024]{1,0:T(8,128)(2,1)S(1)} %get-tuple-element.57), channel_id=1, source_target_pairs={{0,2},{1,3},{2,0},{3,1},{4,6},{5,7},{6,4},{7,5},{8,10},{9,11},{10,... | collective-permute-start | bytes 294920 | tf_op jit(solution)/shard_map/ppermute | solution.py:26
  5.4 32.5 %collective-permute-start.6 = (bf16[48,1024]{1,0:T(8,128)(2,1)S(1)}, bf16[48,1024]{1,0:T(8,128)(2,1)S(1)}, u32[]{:S(2)}, u32[]{:S(2)}) collective-permute-start(bf16[48,1024]{1,0:T(8,128)(2,1)S(1)} %get-tuple-element.56), channel_id=1, source_target_pairs={{0,3},{1,2},{2,1},{3,0},{4,7},{5,6},{6,5},{7,4},{8,11},{9,10},{10,... | collective-permute-start | bytes 294920 | tf_op jit(solution)/shard_map/ppermute | solution.py:26
  13.9 13.4 %collective-permute-start.2 = (bf16[192,1024]{1,0:T(8,128)(2,1)S(1)}, bf16[192,1024]{1,0:T(8,128)(2,1)S(1)}, u32[]{:S(2)}, u32[]{:S(2)}) collective-permute-start(bf16[192,1024]{1,0:T(8,128)(2,1)S(1)} %collective-permute-done.1.rest_2_), channel_id=1, source_target_pairs={{0,1},{1,0},{2,3},{3,2},{4,5},{5,4},{6,7},{7,6},{8,9},{9,8},{10,11... | collective-permute-start | bytes 1179656 | tf_op jit(solution)/shard_map/ppermute | solution.py:26
  13.9 10.2 %copy-start.7 = (s32[3,64]{1,0:T(4,128)S(1)}, s32[3,64]{1,0:T(4,128)}, u32[]{:S(2)}) copy-start(s32[3,64]{1,0:T(4,128)} %param.22) | copy-start | bytes 2308
  13.9 15.9 %copy-start.1 = (bf16[3,64,1024]{2,1,0:T(8,128)(2,1)S(1)}, bf16[3,64,1024]{2,1,0:T(8,128)(2,1)}, u32[]{:S(2)}) copy-start(bf16[3,64,1024]{2,1,0:T(8,128)(2,1)} %param.12) | copy-start | bytes 1179652
  13.9 15.9 %copy-start.4 = (f32[4096]{0:T(1024)S(1)}, f32[4096]{0:T(1024)}, u32[]{:S(2)}) copy-start(f32[4096]{0:T(1024)} %param.14) | copy-start | bytes 49156
  13.9 15.9 %copy-start.5 = (f32[4096]{0:T(1024)S(1)}, f32[4096]{0:T(1024)}, u32[]{:S(2)}) copy-start(f32[4096]{0:T(1024)} %param.15) | copy-start | bytes 49156
  24.1 11.1 %collective-permute-start.3 = (s32[3,64]{1,0:T(4,128)S(1)}, s32[3,64]{1,0:T(4,128)S(1)}, u32[]{:S(2)}, u32[]{:S(2)}) collective-permute-start(s32[3,64]{1,0:T(4,128)S(1)} %copy-done.7), channel_id=1, source_target_pairs={{0,16},{4,20},{8,24},{12,28},{16,0},{20,4},{24,8},{28,12},{1,17},{... | collective-permute-start | bytes 2312 | tf_op jit(solution)/shard_map/ppermute | solution.py:26
  27.2 19.2 %collective-permute-start.10 = (bf16[2,256,256]{2,1,0:T(8,128)(2,1)}, bf16[2,256,256]{2,1,0:T(8,128)(2,1)S(1)}, u32[]{:S(2)}, u32[]{:S(2)}) collective-permute-start(bf16[2,256,256]{2,1,0:T(8,128)(2,1)} %get-tuple-element.33), channel_id=1, source_target_pairs={{0,12},{4,8},{8,4},{12,0},{16,28},{20,24},{24,20},{28,16},{1,13},{... | collective-permute-start | bytes 786440 | tf_op jit(solution)/shard_map/ppermute | solution.py:26
  31.9 3.3 %copy-start.9 = (bf16[2,256,256]{2,1,0:T(8,128)(2,1)S(1)}, bf16[2,256,256]{2,1,0:T(8,128)(2,1)}, u32[]{:S(2)}) copy-start(bf16[2,256,256]{2,1,0:T(8,128)(2,1)} %get-tuple-element.31) | copy-start | bytes 786436
  31.9 3.9 %copy-start.6 = (s32[24,5]{0,1:T(8,128)S(1)}, s32[24,5]{0,1:T(8,128)}, u32[]{:S(2)}) copy-start(s32[24,5]{0,1:T(8,128)} %param.21) | copy-start | bytes 1444
  35.2 14.0 %collective-permute-start.8 = (bf16[2,256,256]{2,1,0:T(8,128)(2,1)S(1)}, bf16[2,256,256]{2,1,0:T(8,128)(2,1)S(1)}, u32[]{:S(2)}, u32[]{:S(2)}) collective-permute-start(bf16[2,256,256]{2,1,0:T(8,128)(2,1)S(1)} %copy-done.9), channel_id=1, source_target_pairs={{0,4},{4,0},{8,12},{12,8},{16,20},{20,16},{24,28},{28,24},{1,5},{5... | collective-permute-start | bytes 786440 | tf_op jit(solution)/shard_map/ppermute | solution.py:26
  36.0 16.0 %collective-permute-start.9 = (bf16[2,256,256]{2,1,0:T(8,128)(2,1)}, bf16[2,256,256]{2,1,0:T(8,128)(2,1)S(1)}, u32[]{:S(2)}, u32[]{:S(2)}) collective-permute-start(bf16[2,256,256]{2,1,0:T(8,128)(2,1)} %get-tuple-element.32), channel_id=1, source_target_pairs={{0,8},{4,12},{8,0},{12,4},{16,24},{20,28},{24,16},{28,20},{1,9},{5... | collective-permute-start | bytes 786440 | tf_op jit(solution)/shard_map/ppermute | solution.py:26
  36.5 31.9 %collective-permute-start.12 = (bf16[2,256,256]{2,1,0:T(8,128)(2,1)}, bf16[2,256,256]{2,1,0:T(8,128)(2,1)S(1)}, u32[]{:S(2)}, u32[]{:S(2)}) collective-permute-start(bf16[2,256,256]{2,1,0:T(8,128)(2,1)} %get-tuple-element.35), channel_id=1, source_target_pairs={{0,4},{4,0},{8,12},{12,8},{16,20},{20,16},{24,28},{28,24},{1,5},{5... | collective-permute-start | bytes 786440 | tf_op jit(solution)/shard_map/ppermute | solution.py:26
  38.0 30.4 %collective-permute-start.13 = (bf16[2,256,256]{2,1,0:T(8,128)(2,1)}, bf16[2,256,256]{2,1,0:T(8,128)(2,1)S(1)}, u32[]{:S(2)}, u32[]{:S(2)}) collective-permute-start(bf16[2,256,256]{2,1,0:T(8,128)(2,1)} %get-tuple-element.36), channel_id=1, source_target_pairs={{0,8},{4,12},{8,0},{12,4},{16,24},{20,28},{24,16},{28,20},{1,9},{5... | collective-permute-start | bytes 786440 | tf_op jit(solution)/shard_map/ppermute | solution.py:26
  39.6 5.1 %copy-start.8 = (s32[72]{0:T(128)S(1)}, s32[72]{0:T(128)}, u32[]{:S(2)}) copy-start(s32[72]{0:T(128)} %owner_ref.1) | copy-start | bytes 868
  39.6 24.2 %copy-start.3 = (bf16[2,256,256]{2,1,0:T(8,128)(2,1)S(1)}, bf16[2,256,256]{2,1,0:T(8,128)(2,1)}, u32[]{:S(2)}) copy-start(bf16[2,256,256]{2,1,0:T(8,128)(2,1)} %get-tuple-element.30.rest_0_) | copy-start | bytes 786436
  40.5 27.8 %copy-start.2 = (bf16[2,256,256]{2,1,0:T(8,128)(2,1)S(1)}, bf16[2,256,256]{2,1,0:T(8,128)(2,1)}, u32[]{:S(2)}) copy-start(bf16[2,256,256]{2,1,0:T(8,128)(2,1)} %get-tuple-element.34.rest_0_) | copy-start | bytes 786436
  40.5 50.1 %all-to-all-start = ((bf16[8,48,512]{2,1,0:T(8,128)(2,1)}), bf16[8,48,512]{2,1,0:T(8,128)(2,1)S(1)}, u32[]{:S(2)}, u32[]{:S(2)}) async-start(bf16[8,48,512]{2,1,0:T(8,128)(2,1)} %bitcast.15), calls=%async_computation | async-start | bytes 786432 | tf_op jit(solution)/shard_map/all_to_all | solution.py:347
  46.4 21.9 %collective-permute-start.14 = (bf16[2,256,256]{2,1,0:T(8,128)(2,1)}, bf16[2,256,256]{2,1,0:T(8,128)(2,1)S(1)}, u32[]{:S(2)}, u32[]{:S(2)}) collective-permute-start(bf16[2,256,256]{2,1,0:T(8,128)(2,1)} %get-tuple-element.37), channel_id=1, source_target_pairs={{0,12},{4,8},{8,4},{12,0},{16,28},{20,24},{24,20},{28,16},{1,13},{... | collective-permute-start | bytes 786440 | tf_op jit(solution)/shard_map/ppermute | solution.py:26
  49.2 14.7 %collective-permute-start.7 = (bf16[192,512]{1,0:T(8,128)(2,1)S(1)}, bf16[192,512]{1,0:T(8,128)(2,1)S(1)}, u32[]{:S(2)}, u32[]{:S(2)}) collective-permute-start(bf16[192,512]{1,0:T(8,128)(2,1)S(1)} %fusion.6.own_query_ref), channel_id=1, source_target_pairs={{0,16},{4,20},{8,24},{12,28},{16,0},{20,4},{24,8},{28,12},{1,17},{... | collective-permute-start | bytes 589832 | tf_op jit(solution)/shard_map/ppermute | solution.py:26
  63.9 21.0 %copy-start = (bf16[4,128,4096]{2,1,0:T(8,128)(2,1)S(1)}, bf16[4,128,4096]{2,1,0:T(8,128)(2,1)}, u32[]{:S(2)}) copy-start(bf16[4,128,4096]{2,1,0:T(8,128)(2,1)} %param.19) | copy-start | bytes 12582916
  64.9 16.9 %collective-permute-start.11 = (bf16[2,192,256]{2,1,0:T(8,128)(2,1)S(1)}, bf16[2,192,256]{2,1,0:T(8,128)(2,1)S(1)}, u32[]{:S(2)}, u32[]{:S(2)}) collective-permute-start(bf16[2,192,256]{2,1,0:T(8,128)(2,1)S(1)} %attend.2.mine_ref), channel_id=1, source_target_pairs={{0,16},{4,20},{8,24},{12,28},{16,0},{20,4},{24,8},{28,12},{1,17},{... | collective-permute-start | bytes 589832 | tf_op jit(solution)/shard_map/ppermute | solution.py:26
  69.4 15.5 %collective-permute-start.15 = (bf16[2,192,256]{2,1,0:T(8,128)(2,1)S(1)}, bf16[2,192,256]{2,1,0:T(8,128)(2,1)S(1)}, u32[]{:S(2)}, u32[]{:S(2)}) collective-permute-start(bf16[2,192,256]{2,1,0:T(8,128)(2,1)S(1)} %attend.3.mine_ref), channel_id=1, source_target_pairs={{0,16},{4,20},{8,24},{12,28},{16,0},{20,4},{24,8},{28,12},{1,17},{... | collective-permute-start | bytes 589832 | tf_op jit(solution)/shard_map/ppermute | solution.py:26
  87.8 4.6 %collective-permute-start.17 = (bf16[192,1024]{1,0:T(8,128)(2,1)S(1)}, bf16[192,1024]{1,0:T(8,128)(2,1)}, u32[]{:S(2)}, u32[]{:S(2)}) collective-permute-start(bf16[192,1024]{1,0:T(8,128)(2,1)S(1)} %get-tuple-element.41), channel_id=1, source_target_pairs={{0,1},{1,0},{2,3},{3,2},{4,5},{5,4},{6,7},{7,6},{8,9},{9,8},{10,11... | collective-permute-start | bytes 1179656 | tf_op jit(solution)/shard_map/ppermute | solution.py:26
  88.5 14.2 %collective-permute-start.26 = (bf16[2,192,256]{2,1,0:T(8,128)(2,1)S(1)}, bf16[2,192,256]{2,1,0:T(8,128)(2,1)S(1)}, u32[]{:S(2)}, u32[]{:S(2)}) collective-permute-start(bf16[2,192,256]{2,1,0:T(8,128)(2,1)S(1)} %join.2.rest_0_), channel_id=1, source_target_pairs={{0,8},{4,12},{8,0},{12,4},{16,24},{20,28},{24,16},{28,20},{1,9},{5... | collective-permute-start | bytes 589832 | tf_op jit(solution)/shard_map/ppermute | solution.py:26
  88.6 15.7 %collective-permute-start.23 = (bf16[2,192,256]{2,1,0:T(8,128)(2,1)S(1)}, bf16[2,192,256]{2,1,0:T(8,128)(2,1)S(1)}, u32[]{:S(2)}, u32[]{:S(2)}) collective-permute-start(bf16[2,192,256]{2,1,0:T(8,128)(2,1)S(1)} %join.3.rest_1_.rest_0_), channel_id=1, source_target_pairs={{0,8},{4,12},{8,0},{12,4},{16,24},{20,28},{24,16},{28,20},{1,9},{5... | collective-permute-start | bytes 589832 | tf_op jit(solution)/shard_map/ppermute | solution.py:26
  90.6 3.2 %collective-permute-start.19 = (bf16[8,48,512]{2,1,0:T(8,128)(2,1)S(1)}, bf16[8,48,512]{2,1,0:T(8,128)(2,1)S(1)}, u32[]{:S(2)}, u32[]{:S(2)}) collective-permute-start(bf16[8,48,512]{2,1,0:T(8,128)(2,1)S(1)} %all-to-all-done), channel_id=1, source_target_pairs={{0,1},{1,0},{2,3},{3,2},{4,5},{5,4},{6,7},{7,6},{8,9},{9,8},{10,11... | collective-permute-start | bytes 1179656 | tf_op jit(solution)/shard_map/ppermute | solution.py:26
  90.6 12.0 %collective-permute-start.20 = (bf16[8,48,512]{2,1,0:T(8,128)(2,1)S(1)}, bf16[8,48,512]{2,1,0:T(8,128)(2,1)S(1)}, u32[]{:S(2)}, u32[]{:S(2)}) collective-permute-start(bf16[8,48,512]{2,1,0:T(8,128)(2,1)S(1)} %all-to-all-done), channel_id=1, source_target_pairs={{0,2},{1,3},{2,0},{3,1},{4,6},{5,7},{6,4},{7,5},{8,10},{9,11},{10,... | collective-permute-start | bytes 1179656 | tf_op jit(solution)/shard_map/ppermute | solution.py:26
  92.4 12.4 %collective-permute-start.16 = (bf16[192,1024]{1,0:T(8,128)(2,1)S(1)}, bf16[192,1024]{1,0:T(8,128)(2,1)S(1)}, u32[]{:S(2)}, u32[]{:S(2)}) collective-permute-start(bf16[192,1024]{1,0:T(8,128)(2,1)S(1)} %get-tuple-element.39), channel_id=1, source_target_pairs={{0,1},{1,0},{2,3},{3,2},{4,5},{5,4},{6,7},{7,6},{8,9},{9,8},{10,11... | collective-permute-start | bytes 1179656 | tf_op jit(solution)/shard_map/ppermute | solution.py:26
  93.8 16.8 %collective-permute-start.18 = (bf16[192,1024]{1,0:T(8,128)(2,1)S(1)}, bf16[192,1024]{1,0:T(8,128)(2,1)S(1)}, u32[]{:S(2)}, u32[]{:S(2)}) collective-permute-start(bf16[192,1024]{1,0:T(8,128)(2,1)S(1)} %add_convert_fusion.1), channel_id=1, source_target_pairs={{0,2},{1,3},{2,0},{3,1},{4,6},{5,7},{6,4},{7,5},{8,10},{9,11},{10,... | collective-permute-start | bytes 1179656 | tf_op jit(solution)/shard_map/ppermute | solution.py:26
  102.6 10.5 %collective-permute-start.21 = (bf16[8,48,512]{2,1,0:T(8,128)(2,1)S(1)}, bf16[8,48,512]{2,1,0:T(8,128)(2,1)S(1)}, u32[]{:S(2)}, u32[]{:S(2)}) collective-permute-start(bf16[8,48,512]{2,1,0:T(8,128)(2,1)S(1)} %collective-permute-done.20), channel_id=1, source_target_pairs={{0,1},{1,0},{2,3},{3,2},{4,5},{5,4},{6,7},{7,6},{8,9},{9,8},{10,11... | collective-permute-start | bytes 1179656 | tf_op jit(solution)/shard_map/ppermute | solution.py:26
  102.7 10.5 %collective-permute-start.25 = (bf16[2,192,256]{2,1,0:T(8,128)(2,1)S(1)}, bf16[2,192,256]{2,1,0:T(8,128)(2,1)S(1)}, u32[]{:S(2)}, u32[]{:S(2)}) collective-permute-start(bf16[2,192,256]{2,1,0:T(8,128)(2,1)S(1)} %join.2.rest_0_), channel_id=1, source_target_pairs={{0,4},{4,0},{8,12},{12,8},{16,20},{20,16},{24,28},{28,24},{1,5},{5... | collective-permute-start | bytes 589832 | tf_op jit(solution)/shard_map/ppermute | solution.py:26
  104.3 15.9 %collective-permute-start.22 = (bf16[2,192,256]{2,1,0:T(8,128)(2,1)S(1)}, bf16[2,192,256]{2,1,0:T(8,128)(2,1)S(1)}, u32[]{:S(2)}, u32[]{:S(2)}) collective-permute-start(bf16[2,192,256]{2,1,0:T(8,128)(2,1)S(1)} %join.3.rest_1_.rest_0_), channel_id=1, source_target_pairs={{0,4},{4,0},{8,12},{12,8},{16,20},{20,16},{24,28},{28,24},{1,5},{5... | collective-permute-start | bytes 589832 | tf_op jit(solution)/shard_map/ppermute | solution.py:26
  104.8 14.2 %collective-permute-start.27 = (bf16[2,192,256]{2,1,0:T(8,128)(2,1)S(1)}, bf16[2,192,256]{2,1,0:T(8,128)(2,1)S(1)}, u32[]{:S(2)}, u32[]{:S(2)}) collective-permute-start(bf16[2,192,256]{2,1,0:T(8,128)(2,1)S(1)} %collective-permute-done.26.rest_2_), channel_id=1, source_target_pairs={{0,4},{4,0},{8,12},{12,8},{16,20},{20,16},{24,28},{28,24},{1,5},{5... | collective-permute-start | bytes 589832 | tf_op jit(solution)/shard_map/ppermute | solution.py:26
  110.6 12.1 %collective-permute-start.24 = (bf16[2,192,256]{2,1,0:T(8,128)(2,1)S(1)}, bf16[2,192,256]{2,1,0:T(8,128)(2,1)S(1)}, u32[]{:S(2)}, u32[]{:S(2)}) collective-permute-start(bf16[2,192,256]{2,1,0:T(8,128)(2,1)S(1)} %collective-permute-done.23.rest_2_), channel_id=1, source_target_pairs={{0,4},{4,0},{8,12},{12,8},{16,20},{20,16},{24,28},{28,24},{1,5},{5... | collective-permute-start | bytes 589832 | tf_op jit(solution)/shard_map/ppermute | solution.py:26

commit v2 on v1

--- a/solution.py
+++ b/solution.py
@@ -66,9 +66,11 @@
     return [blocks[j] for j in range(size)]
 
 
-def pairs_kernel(chunks, heads, groups, capacity, splits, me_ref, refs_ref, owner_ref, latent_hbm, weight_hbm, *rest):
+def pairs_kernel(chunks, heads, groups, capacity, splits, refs_hbm, owner_hbm, latent_hbm, weight_hbm, *rest):
     half = groups // 2
-    outs, (latent_buf, weight_buf, acc, pairs, picked, sems) = rest[: half * chunks], rest[half * chunks :]
+    outs = rest[: half * chunks]
+    latent_buf, weight_buf, acc, pairs, refs_ref, owner_ref, picked, sems, table_sems = rest[half * chunks :]
+    me = lax.axis_index("dp")
     images_local, latent_rows = pairs.shape[1], pairs.shape[2]
     depth = latent_hbm.shape[1] // splits
     copies = []
@@ -79,7 +81,16 @@
         latent_copy.start()
         copies.append((weight_copy, latent_copy))
 
-    low = me_ref[0] * images_local
+    tables = (
+        pltpu.make_async_copy(refs_hbm, refs_ref, table_sems.at[0]),
+        pltpu.make_async_copy(owner_hbm, owner_ref, table_sems.at[1]),
+    )
+    for table in tables:
+        table.start()
+    for table in tables:
+        table.wait()
+
+    low = me * images_local
     per_sequence = refs_ref.shape[0]
     sequences = refs_ref.shape[1] // groups
 
@@ -89,7 +100,7 @@
         count = 0
         for sequence in range(sequences):
             for position in range(per_sequence):
-                image = refs_ref[position, (me_ref[0] ^ offset) * sequences + sequence]
+                image = refs_ref[position, (me ^ offset) * sequences + sequence]
                 within = owner_ref[jnp.maximum(image, 0)] - low
                 hit = (image >= 0) & (within >= 0) & (within < images_local)
                 slot = jnp.where(hit, jnp.minimum(count, capacity - 1), capacity)
@@ -125,7 +136,7 @@
         copy.wait()
 
 
-def outgoing_pairs(me, media_refs, owner_map, latents, weight, groups, capacity, chunks):
+def outgoing_pairs(media_refs, owner_map, latents, weight, groups, capacity, chunks):
     images_local, latent_rows, model_width = latents.shape
     heads, width = weight.shape[1:]
     rows = images_local * latent_rows
@@ -137,21 +148,24 @@
     outs = pl.pallas_call(
         functools.partial(pairs_kernel, chunks, heads, groups, capacity, splits),
         out_shape=[jax.ShapeDtypeStruct(shape, BF16)] * (half * chunks),
-        in_specs=[SMEM, SMEM, SMEM, hbm, hbm],
+        in_specs=[hbm] * 4,
         out_specs=[hbm] * (half * chunks),
         scratch_shapes=[
             pltpu.VMEM((splits, rows, depth), BF16),
             pltpu.VMEM((splits, depth, heads, width), BF16),
             pltpu.VMEM((heads, rows, width), F32),
             pltpu.VMEM((heads, images_local, latent_rows, width), BF16),
+            pltpu.SMEM(media_refs.shape[::-1], jnp.int32),
+            pltpu.SMEM(owner_map.shape, jnp.int32),
             pltpu.SMEM((groups * (capacity + 1),), jnp.int32),
             pltpu.SemaphoreType.DMA((2 * splits + groups * capacity * heads,)),
+            pltpu.SemaphoreType.DMA((2,)),
         ],
         cost_estimate=pl.CostEstimate(
             flops=2 * rows * model_width * heads * width, bytes_accessed=latents.size * 2 + weight.size * 2, transcendentals=0
         ),
         name="pairs",
-    )(me.reshape(1), media_refs.T, owner_map, latents.reshape(rows, model_width), weight)
+    )(media_refs.T, owner_map, latents.reshape(rows, model_width), weight)
     return [outs[chunk * half : (chunk + 1) * half] for chunk in range(chunks)]
 
 
@@ -237,7 +251,6 @@
         out_specs=[VMEM] * shards,
         out_shape=[jax.ShapeDtypeStruct((tokens, feats), BF16)] * shards,
         scratch_shapes=[pltpu.VMEM((shards, weight.shape[0], feats), BF16), pltpu.SemaphoreType.DMA((shards,))],
-        compiler_params=limit(20),
         name="update",
     )(place, weight, *contexts)
 
@@ -303,7 +316,7 @@
 
     far_pos = swap(media_pos, "dp", half)
     text_blocks = gather_blocks(text_states.reshape(tokens, feat_local), "fsdp")
-    outgoing = outgoing_pairs(me, media_refs, owner_map, latents, latent_weight, groups, capacity, chunks)
+    outgoing = outgoing_pairs(media_refs, owner_map, latents, latent_weight, groups, capacity, chunks)
     arrived = []
     for chunk in range(chunks):
         received = {o: swap(outgoing[chunk][o], "dp", o) for o in range(half - 1, 0, -1)}

time: 125 us -> 127 us (1.016)
  local copies, waits for them, and re-layouts: 3.24 us -> 4.63 us
    pallas_call x1, Pallas kernels: 2.9 us -> 4.62 us  [update_terms(): pl.pallas_call(functools.partial(update_kernel, shards, len(contexts)), i...]
    unnamed x20 -> x36, local copies, waits for them, and re-layouts: 0.05 us -> 1.45 us
  transfers between devices with their start and end apart: 29 -> 29, of which waited for: 8 -> 8; matrix products, arithmetic and copies ran while one was open for 8% -> 7% of each run, Pallas kernels for 15% -> 15%
where the time goes in v2:
time: 127 us
  waiting for transfers between devices  55.1 us (43%)
  starting transfers between devices  37.3 us (29%)
  Pallas kernels  21.6 us (17%)
  local copies, waits for them, and re-layouts  4.63 us (4%)
  matrix products  3.3 us (3%)
  other arithmetic  2.95 us (2%)
  between operations  1.85 us (1%)
    ppermute x28, waiting for transfers between devices, swap(): return lax.ppermute(value, axis, [(i, i ^ offset) for i in range(size)])  55.1 us
    ppermute x28, starting transfers between devices, swap(): return lax.ppermute(value, axis, [(i, i ^ offset) for i in range(size)])  33.6 us
    pallas_call x1, Pallas kernels, outgoing_pairs(): pl.pallas_call(functools.partial(pairs_kernel, chunks, heads, groups, cap...  9.37 us
    pallas_call x1, Pallas kernels, update_terms(): pl.pallas_call(functools.partial(update_kernel, shards, len(contexts)), i...  4.62 us
    all_to_all x1, starting transfers between devices, body(): lax.all_to_all(share_rows.reshape(groups, share, cols), 'dp', 0, 0, tiled...  3.76 us
    pallas_call x2, Pallas kernels, grad_part(): pl.pallas_call(functools.partial(grad_kernel, count), out_shape=jax.Shape...  3.36 us
    dot_general x1, matrix products, body(): jnp.dot(normed, query_weight.reshape(model_width, head_local * head_size)...  3.3 us
  transfers between devices with their start and end apart: 29, of which 8 were waited for; matrix products, arithmetic and copies ran while one was open for 7% of the time, Pallas kernels for 15%

profile of v2, /device:TPU:0, one launch (start us, length us, event | category | flops | bytes accessed | tf_op | source)
XLA Modules:
  0.0 126.7 jit_solution(14666717993116389027)
XLA Ops:
  0.6 3.1 %collective-permute-start.1 = (bf16[192,1024]{1,0:T(8,128)(2,1)}, bf16[192,1024]{1,0:T(8,128)(2,1)S(1)}, u32[]{:S(2)}, u32[]{:S(2)}) collective-permute-start(bf16[192,1024]{1,0:T(8,128)(2,1)} %bitcast.48), channel_id=1, source_target_pairs={{0,2},{1,3},{2,0},{3,1},{4,6},{5,7},{6,4},{7,5},{8,10},{9,11},{10,... | collective-permute-start | bytes 1179656 | tf_op jit(solution)/shard_map/ppermute | solution.py:26
  3.7 1.1 constant_dynamic-slice_fusion
  4.8 0.6 collective-permute-start.4
  5.4 1.3 %collective-permute-start.6 = (bf16[48,1024]{1,0:T(8,128)(2,1)S(1)}, bf16[48,1024]{1,0:T(8,128)(2,1)S(1)}, u32[]{:S(2)}, u32[]{:S(2)}) collective-permute-start(bf16[48,1024]{1,0:T(8,128)(2,1)S(1)} %get-tuple-element.56), channel_id=1, source_target_pairs={{0,3},{1,2},{2,1},{3,0},{4,7},{5,6},{6,5},{7,4},{8,11},{9,10},{10,... | collective-permute-start | bytes 294920 | tf_op jit(solution)/shard_map/ppermute | solution.py:26
  6.8 7.0 %collective-permute-done.1.rest_2_ = bf16[192,1024]{1,0:T(8,128)(2,1)S(1)} collective-permute-done((bf16[192,1024]{1,0:T(8,128)(2,1)}, bf16[192,1024]{1,0:T(8,128)(2,1)S(1)}, u32[]{:S(2)}, u32[]{:S(2)}) %collective-permute-start.1) | collective-permute-done | bytes 393248 | tf_op jit(solution)/shard_map/ppermute | solution.py:26
  13.9 9.4 %pairs.1 = (bf16[2,256,256]{2,1,0:T(8,128)(2,1)}, bf16[2,256,256]{2,1,0:T(8,128)(2,1)}, bf16[2,256,256]{2,1,0:T(8,128)(2,1)}, bf16[2,256,256]{2,1,0:T(8,128)(2,1...) custom-call(s32[5,24]{1,0:T(8,128)} %bitcast.57, ...), custom_call_target="tpu_custom_call" | custom-call | flops 4831838208 | bytes 13107200 | tf_op jit(solution)/shard_map/pairs/pallas_call | solution.py:148
  23.3 3.1 %collective-permute-start.3 = (s32[3,64]{1,0:T(4,128)S(1)}, s32[3,64]{1,0:T(4,128)S(1)}, u32[]{:S(2)}, u32[]{:S(2)}) collective-permute-start(s32[3,64]{1,0:T(4,128)S(1)} %copy-done.14), channel_id=1, source_target_pairs={{0,16},{4,20},{8,24},{12,28},{16,0},{20,4},{24,8},{28,12},{1,17},{... | collective-permute-start | bytes 2312 | tf_op jit(solution)/shard_map/ppermute | solution.py:26
  26.4 2.5 %collective-permute-start.10 = (bf16[2,256,256]{2,1,0:T(8,128)(2,1)}, bf16[2,256,256]{2,1,0:T(8,128)(2,1)S(1)}, u32[]{:S(2)}, u32[]{:S(2)}) collective-permute-start(bf16[2,256,256]{2,1,0:T(8,128)(2,1)} %get-tuple-element.33), channel_id=1, source_target_pairs={{0,12},{4,8},{8,4},{12,0},{16,28},{20,24},{24,20},{28,16},{1,13},{... | collective-permute-start | bytes 786440 | tf_op jit(solution)/shard_map/ppermute | solution.py:26
  29.0 2.1 %norm.1 = bf16[192,4096]{1,0:T(8,128)(2,1)S(1)} custom-call(s32[2]{0:T(128)S(1)} %pad_add_fusion.place_ref, f32[1,4096]{1,0:T(1,128)S(1)} %bitcast.51, f32[1,4096]{1,0:T(1,128)S(1)} %bitcast.52, bf16[192,1024]{1,0:T(8,128)(2,1)S(1)} %bitcast.50, bf16[192,1024]{1,0:T(8,128)(2,1)S(1)} %collective-permute-done.rest_1_, ...), custom_call_target="tpu_custom_call" | custom-call | tf_op jit(solution)/shard_map/norm/pallas_call | solution.py:48
  31.1 3.3 %fusion.6.own_query_ref = bf16[192,512]{1,0:T(8,128)(2,1)S(1)} fusion(bf16[192,4096]{1,0:T(8,128)(2,1)S(1)} %norm.1, bf16[512,8,4,128]{3,2,1,0:T(4,128)(2,1)} %bitcast.59), kind=kOutput, calls=%fused_computation.4 | convolution fusion | flops 805502976 | bytes 5963776 | tf_op jit(solution)/shard_map/dot_general | solution.py:326
  34.5 0.6 collective-permute-start.8
  35.2 0.5 collective-permute-start.9
  35.7 1.5 %collective-permute-start.12 = (bf16[2,256,256]{2,1,0:T(8,128)(2,1)}, bf16[2,256,256]{2,1,0:T(8,128)(2,1)S(1)}, u32[]{:S(2)}, u32[]{:S(2)}) collective-permute-start(bf16[2,256,256]{2,1,0:T(8,128)(2,1)} %get-tuple-element.35), channel_id=1, source_target_pairs={{0,4},{4,0},{8,12},{12,8},{16,20},{20,16},{24,28},{28,24},{1,5},{5... | collective-permute-start | bytes 786440 | tf_op jit(solution)/shard_map/ppermute | solution.py:26
  37.2 1.6 %collective-permute-start.13 = (bf16[2,256,256]{2,1,0:T(8,128)(2,1)}, bf16[2,256,256]{2,1,0:T(8,128)(2,1)S(1)}, u32[]{:S(2)}, u32[]{:S(2)}) collective-permute-start(bf16[2,256,256]{2,1,0:T(8,128)(2,1)} %get-tuple-element.36), channel_id=1, source_target_pairs={{0,8},{4,12},{8,0},{12,4},{16,24},{20,28},{24,16},{28,20},{1,9},{5... | collective-permute-start | bytes 786440 | tf_op jit(solution)/shard_map/ppermute | solution.py:26
  39.0 0.8 pad_maximum_fusion
  39.7 3.8 %all-to-all-start = ((bf16[8,48,512]{2,1,0:T(8,128)(2,1)}), bf16[8,48,512]{2,1,0:T(8,128)(2,1)S(1)}, u32[]{:S(2)}, u32[]{:S(2)}) async-start(bf16[8,48,512]{2,1,0:T(8,128)(2,1)} %bitcast.15), calls=%async_computation | async-start | bytes 786432 | tf_op jit(solution)/shard_map/all_to_all | solution.py:360
  43.5 0.1 copy.32
  43.6 0.1 max.21
  43.7 0.1 copy.35
  43.8 0.1 max.23
  43.9 0.2 select_reduce_fusion.2
  44.1 0.1 copy.33
  44.2 0.1 ge.28
  44.3 0.2 convert_reduce_fusion.1
  44.5 0.1 reduce_sum.60
  44.6 0.1 and.62
  44.7 0.1 copy.36
  44.9 0.1 ge.31
  44.9 0.2 convert_reduce_fusion
  45.1 0.1 reduce_sum.64
  45.3 0.1 and.67
  45.4 0.1 copy.34
  45.6 0.1 copy.37
  45.7 2.7 %collective-permute-start.14 = (bf16[2,256,256]{2,1,0:T(8,128)(2,1)}, bf16[2,256,256]{2,1,0:T(8,128)(2,1)S(1)}, u32[]{:S(2)}, u32[]{:S(2)}) collective-permute-start(bf16[2,256,256]{2,1,0:T(8,128)(2,1)} %get-tuple-element.37), channel_id=1, source_target_pairs={{0,12},{4,8},{8,4},{12,0},{16,28},{20,24},{24,20},{28,16},{1,13},{... | collective-permute-start | bytes 786440 | tf_op jit(solution)/shard_map/ppermute | solution.py:26
  48.4 2.5 %collective-permute-start.7 = (bf16[192,512]{1,0:T(8,128)(2,1)S(1)}, bf16[192,512]{1,0:T(8,128)(2,1)S(1)}, u32[]{:S(2)}, u32[]{:S(2)}) collective-permute-start(bf16[192,512]{1,0:T(8,128)(2,1)S(1)} %fusion.6.own_query_ref), channel_id=1, source_target_pairs={{0,16},{4,20},{8,24},{12,28},{16,0},{20,4},{24,8},{28,12},{1,17},{... | collective-permute-start | bytes 589832 | tf_op jit(solution)/shard_map/ppermute | solution.py:26
  50.9 0.1 reshape.202.own_slot_ref
  51.0 0.1 reshape.203.far_slot_ref
  51.2 11.9 %collective-permute-done.7.far_query_ref = bf16[192,512]{1,0:T(8,128)(2,1)S(1)} collective-permute-done((bf16[192,512]{1,0:T(8,128)(2,1)S(1)}, bf16[192,512]{1,0:T(8,128)(2,1)S(1)}, u32[]{:S(2)}, u32[]{:S(2)}) %collective-permute-start.7) | collective-permute-done | bytes 196640 | tf_op jit(solution)/shard_map/ppermute | solution.py:26
  63.1 1.0 attend.2.mine_ref
  64.1 3.4 %collective-permute-start.11 = (bf16[2,192,256]{2,1,0:T(8,128)(2,1)S(1)}, bf16[2,192,256]{2,1,0:T(8,128)(2,1)S(1)}, u32[]{:S(2)}, u32[]{:S(2)}) collective-permute-start(bf16[2,192,256]{2,1,0:T(8,128)(2,1)S(1)} %attend.2.mine_ref), channel_id=1, source_target_pairs={{0,16},{4,20},{8,24},{12,28},{16,0},{20,4},{24,8},{28,12},{1,17},{... | collective-permute-start | bytes 589832 | tf_op jit(solution)/shard_map/ppermute | solution.py:26
  67.6 1.0 attend.3.mine_ref
  68.6 0.1 collective-permute-start.15
  68.7 12.4 %collective-permute-done.11.other_ref = bf16[2,192,256]{2,1,0:T(8,128)(2,1)S(1)} collective-permute-done((bf16[2,192,256]{2,1,0:T(8,128)(2,1)S(1)}, bf16[2,192,256]{2,1,0:T(8,128)(2,1)S(1)}, u32[]{:S(2)}, u32[]{:S(2)}) %collective-permute-start.11) | collective-permute-done | bytes 196640 | tf_op jit(solution)/shard_map/ppermute | solution.py:26
  81.1 0.7 copy-done.2
  81.8 2.3 %collective-permute-done.15.other_ref = bf16[2,192,256]{2,1,0:T(8,128)(2,1)S(1)} collective-permute-done((bf16[2,192,256]{2,1,0:T(8,128)(2,1)S(1)}, bf16[2,192,256]{2,1,0:T(8,128)(2,1)S(1)}, u32[]{:S(2)}, u32[]{:S(2)}) %collective-permute-start.15) | collective-permute-done | bytes 196640 | tf_op jit(solution)/shard_map/ppermute | solution.py:26
  84.1 0.7 copy-done
  84.8 4.6 %update.1 = (bf16[192,1024]{1,0:T(8,128)(2,1)}, bf16[192,1024]{1,0:T(8,128)(2,1)}, bf16[192,1024]{1,0:T(8,128)(2,1)}, bf16[192,1024]{1,0:T(8,128)(2,1)}) custom-call(s32[2]{0:T(128)} %copy-done.9, bf16[512,4096]{1,0:T(8,128)(2,1)} %bitcast.53, bf16[2,192,256]{2,1,0:T(8,128)(2,1)} %copy-done.2, bf16[2,192,256]{2,1,0:T(8,128)(2,1)} %copy-done), custom_call_target="tpu_custom_call" | custom-call | tf_op jit(solution)/shard_map/update/pallas_call | solution.py:248
  90.4 2.0 %collective-permute-start.23 = (bf16[2,192,256]{2,1,0:T(8,128)(2,1)S(1)}, bf16[2,192,256]{2,1,0:T(8,128)(2,1)S(1)}, u32[]{:S(2)}, u32[]{:S(2)}) collective-permute-start(bf16[2,192,256]{2,1,0:T(8,128)(2,1)S(1)} %copy-done.1), channel_id=1, source_target_pairs={{0,8},{4,12},{8,0},{12,4},{16,24},{20,28},{24,16},{28,20},{1,9},{5... | collective-permute-start | bytes 589832 | tf_op jit(solution)/shard_map/ppermute | solution.py:26
  92.4 1.5 %collective-permute-start.20 = (bf16[8,48,512]{2,1,0:T(8,128)(2,1)S(1)}, bf16[8,48,512]{2,1,0:T(8,128)(2,1)S(1)}, u32[]{:S(2)}, u32[]{:S(2)}) collective-permute-start(bf16[8,48,512]{2,1,0:T(8,128)(2,1)S(1)} %all-to-all-done), channel_id=1, source_target_pairs={{0,2},{1,3},{2,0},{3,1},{4,6},{5,7},{6,4},{7,5},{8,10},{9,11},{10,... | collective-permute-start | bytes 1179656 | tf_op jit(solution)/shard_map/ppermute | solution.py:26
  93.9 0.2 broadcast_in_dim.87
  94.2 0.3 collective-permute-start.16
  94.5 0.1 add_convert_fusion.1
  94.6 1.0 collective-permute-start.18
  95.6 8.8 %collective-permute-done.20 = bf16[8,48,512]{2,1,0:T(8,128)(2,1)S(1)} collective-permute-done((bf16[8,48,512]{2,1,0:T(8,128)(2,1)S(1)}, bf16[8,48,512]{2,1,0:T(8,128)(2,1)S(1)}, u32[]{:S(2)}, u32[]{:S(2)}) %collective-permute-start.20) | collective-permute-done | bytes 393248 | tf_op jit(solution)/shard_map/ppermute | solution.py:26
  104.5 1.5 %collective-permute-start.25 = (bf16[2,192,256]{2,1,0:T(8,128)(2,1)S(1)}, bf16[2,192,256]{2,1,0:T(8,128)(2,1)S(1)}, u32[]{:S(2)}, u32[]{:S(2)}) collective-permute-start(bf16[2,192,256]{2,1,0:T(8,128)(2,1)S(1)} %copy-done.3), channel_id=1, source_target_pairs={{0,4},{4,0},{8,12},{12,8},{16,20},{20,16},{24,28},{28,24},{1,5},{5... | collective-permute-start | bytes 589832 | tf_op jit(solution)/shard_map/ppermute | solution.py:26
  106.0 0.5 collective-permute-start.22
  106.6 1.5 %collective-permute-start.27 = (bf16[2,192,256]{2,1,0:T(8,128)(2,1)S(1)}, bf16[2,192,256]{2,1,0:T(8,128)(2,1)S(1)}, u32[]{:S(2)}, u32[]{:S(2)}) collective-permute-start(bf16[2,192,256]{2,1,0:T(8,128)(2,1)S(1)} %collective-permute-done.26.rest_2_), channel_id=1, source_target_pairs={{0,4},{4,0},{8,12},{12,8},{16,20},{20,16},{24,28},{28,24},{1,5},{5... | collective-permute-start | bytes 589832 | tf_op jit(solution)/shard_map/ppermute | solution.py:26
  108.1 4.3 %collective-permute-done.18 = bf16[192,1024]{1,0:T(8,128)(2,1)S(1)} collective-permute-done((bf16[192,1024]{1,0:T(8,128)(2,1)S(1)}, bf16[192,1024]{1,0:T(8,128)(2,1)S(1)}, u32[]{:S(2)}, u32[]{:S(2)}) %collective-permute-start.18) | collective-permute-done | bytes 393248 | tf_op jit(solution)/shard_map/ppermute | solution.py:26
  112.3 1.5 %collective-permute-start.24 = (bf16[2,192,256]{2,1,0:T(8,128)(2,1)S(1)}, bf16[2,192,256]{2,1,0:T(8,128)(2,1)S(1)}, u32[]{:S(2)}, u32[]{:S(2)}) collective-permute-start(bf16[2,192,256]{2,1,0:T(8,128)(2,1)S(1)} %collective-permute-done.23.rest_2_), channel_id=1, source_target_pairs={{0,4},{4,0},{8,12},{12,8},{16,20},{20,16},{24,28},{28,24},{1,5},{5... | collective-permute-start | bytes 589832 | tf_op jit(solution)/shard_map/ppermute | solution.py:26
  113.8 1.0 add_convert_fusion
  114.9 5.8 %collective-permute-done.27.rest_3_ = bf16[2,192,256]{2,1,0:T(8,128)(2,1)S(1)} collective-permute-done((bf16[2,192,256]{2,1,0:T(8,128)(2,1)S(1)}, bf16[2,192,256]{2,1,0:T(8,128)(2,1)S(1)}, u32[]{:S(2)}, u32[]{:S(2)}) %collective-permute-start.27) | collective-permute-done | bytes 196640 | tf_op jit(solution)/shard_map/ppermute | solution.py:26
  120.8 1.2 grad.2.rest_4_
  122.0 2.5 %collective-permute-done.24.rest_3_ = bf16[2,192,256]{2,1,0:T(8,128)(2,1)S(1)} collective-permute-done((bf16[2,192,256]{2,1,0:T(8,128)(2,1)S(1)}, bf16[2,192,256]{2,1,0:T(8,128)(2,1)S(1)}, u32[]{:S(2)}, u32[]{:S(2)}) %collective-permute-start.24) | collective-permute-done | bytes 196640 | tf_op jit(solution)/shard_map/ppermute | solution.py:26
  124.5 2.2 %grad.3 = f32[512,512]{1,0:T(8,128)} custom-call(s32[2]{0:T(128)S(1)} %copy-done.10, f32[1]{0:T(128)} %tanh.3.gate_ref, bf16[1536,512]{1,0:T(8,128)(2,1)S(1)} %bitcast.47, bf16[2,192,256]{2,1,0:T(8,128)(2,1)S(1)} %copy-done.1, bf16[2,192,256]{2,1,0:T(8,128)(2,1)S(1)} %collective-permute-done.22.rest_1_, ...), custom_call_target="tpu_custom_call" | custom-call | tf_op jit(solution)/shard_map/grad/pallas_call | solution.py:276
  (86 shorter events, 1.3 us)
Async XLA Ops:
  0.6 13.2 %collective-permute-start.1 = (bf16[192,1024]{1,0:T(8,128)(2,1)}, bf16[192,1024]{1,0:T(8,128)(2,1)S(1)}, u32[]{:S(2)}, u32[]{:S(2)}) collective-permute-start(bf16[192,1024]{1,0:T(8,128)(2,1)} %bitcast.48), channel_id=1, source_target_pairs={{0,2},{1,3},{2,0},{3,1},{4,6},{5,7},{6,4},{7,5},{8,10},{9,11},{10,... | collective-permute-start | bytes 1179656 | tf_op jit(solution)/shard_map/ppermute | solution.py:26
  3.7 19.6 %collective-permute-start = (bf16[192,1024]{1,0:T(8,128)(2,1)}, bf16[192,1024]{1,0:T(8,128)(2,1)S(1)}, u32[]{:S(2)}, u32[]{:S(2)}) collective-permute-start(bf16[192,1024]{1,0:T(8,128)(2,1)} %bitcast.49), channel_id=1, source_target_pairs={{0,1},{1,0},{2,3},{3,2},{4,5},{5,4},{6,7},{7,6},{8,9},{9,8},{10,11... | collective-permute-start | bytes 1179656 | tf_op jit(solution)/shard_map/ppermute | solution.py:26
  4.8 30.4 %collective-permute-start.4 = (bf16[48,1024]{1,0:T(8,128)(2,1)S(1)}, bf16[48,1024]{1,0:T(8,128)(2,1)S(1)}, u32[]{:S(2)}, u32[]{:S(2)}) collective-permute-start(bf16[48,1024]{1,0:T(8,128)(2,1)S(1)} %get-tuple-element.58), channel_id=1, source_target_pairs={{0,1},{1,0},{2,3},{3,2},{4,5},{5,4},{6,7},{7,6},{8,9},{9,8},{10,11... | collective-permute-start | bytes 294920 | tf_op jit(solution)/shard_map/ppermute | solution.py:26
  5.3 30.4 %collective-permute-start.5 = (bf16[48,1024]{1,0:T(8,128)(2,1)S(1)}, bf16[48,1024]{1,0:T(8,128)(2,1)S(1)}, u32[]{:S(2)}, u32[]{:S(2)}) collective-permute-start(bf16[48,1024]{1,0:T(8,128)(2,1)S(1)} %get-tuple-element.57), channel_id=1, source_target_pairs={{0,2},{1,3},{2,0},{3,1},{4,6},{5,7},{6,4},{7,5},{8,10},{9,11},{10,... | collective-permute-start | bytes 294920 | tf_op jit(solution)/shard_map/ppermute | solution.py:26
  5.4 31.8 %collective-permute-start.6 = (bf16[48,1024]{1,0:T(8,128)(2,1)S(1)}, bf16[48,1024]{1,0:T(8,128)(2,1)S(1)}, u32[]{:S(2)}, u32[]{:S(2)}) collective-permute-start(bf16[48,1024]{1,0:T(8,128)(2,1)S(1)} %get-tuple-element.56), channel_id=1, source_target_pairs={{0,3},{1,2},{2,1},{3,0},{4,7},{5,6},{6,5},{7,4},{8,11},{9,10},{10,... | collective-permute-start | bytes 294920 | tf_op jit(solution)/shard_map/ppermute | solution.py:26
  6.8 22.1 %copy-start.9 = (s32[2]{0:T(128)}, s32[2]{0:T(128)S(1)}, u32[]{:S(2)}) copy-start(s32[2]{0:T(128)S(1)} %pad_add_fusion.place_ref) | copy-start | bytes 28
  13.9 12.6 %collective-permute-start.2 = (bf16[192,1024]{1,0:T(8,128)(2,1)S(1)}, bf16[192,1024]{1,0:T(8,128)(2,1)S(1)}, u32[]{:S(2)}, u32[]{:S(2)}) collective-permute-start(bf16[192,1024]{1,0:T(8,128)(2,1)S(1)} %collective-permute-done.1.rest_2_), channel_id=1, source_target_pairs={{0,1},{1,0},{2,3},{3,2},{4,5},{5,4},{6,7},{7,6},{8,9},{9,8},{10,11... | collective-permute-start | bytes 1179656 | tf_op jit(solution)/shard_map/ppermute | solution.py:26
  13.9 9.4 %copy-start.14 = (s32[3,64]{1,0:T(4,128)S(1)}, s32[3,64]{1,0:T(4,128)}, u32[]{:S(2)}) copy-start(s32[3,64]{1,0:T(4,128)} %param.22) | copy-start | bytes 2308
  13.9 15.1 %copy-start.4 = (bf16[3,64,1024]{2,1,0:T(8,128)(2,1)S(1)}, bf16[3,64,1024]{2,1,0:T(8,128)(2,1)}, u32[]{:S(2)}) copy-start(bf16[3,64,1024]{2,1,0:T(8,128)(2,1)} %param.12) | copy-start | bytes 1179652
  13.9 15.1 %copy-start.7 = (f32[4096]{0:T(1024)S(1)}, f32[4096]{0:T(1024)}, u32[]{:S(2)}) copy-start(f32[4096]{0:T(1024)} %param.14) | copy-start | bytes 49156
  13.9 15.1 %copy-start.8 = (f32[4096]{0:T(1024)S(1)}, f32[4096]{0:T(1024)}, u32[]{:S(2)}) copy-start(f32[4096]{0:T(1024)} %param.15) | copy-start | bytes 49156
  23.3 11.1 %collective-permute-start.3 = (s32[3,64]{1,0:T(4,128)S(1)}, s32[3,64]{1,0:T(4,128)S(1)}, u32[]{:S(2)}, u32[]{:S(2)}) collective-permute-start(s32[3,64]{1,0:T(4,128)S(1)} %copy-done.14), channel_id=1, source_target_pairs={{0,16},{4,20},{8,24},{12,28},{16,0},{20,4},{24,8},{28,12},{1,17},{... | collective-permute-start | bytes 2312 | tf_op jit(solution)/shard_map/ppermute | solution.py:26
  26.4 19.2 %collective-permute-start.10 = (bf16[2,256,256]{2,1,0:T(8,128)(2,1)}, bf16[2,256,256]{2,1,0:T(8,128)(2,1)S(1)}, u32[]{:S(2)}, u32[]{:S(2)}) collective-permute-start(bf16[2,256,256]{2,1,0:T(8,128)(2,1)} %get-tuple-element.33), channel_id=1, source_target_pairs={{0,12},{4,8},{8,4},{12,0},{16,28},{20,24},{24,20},{28,16},{1,13},{... | collective-permute-start | bytes 786440 | tf_op jit(solution)/shard_map/ppermute | solution.py:26
  31.1 3.3 %copy-start.17 = (bf16[2,256,256]{2,1,0:T(8,128)(2,1)S(1)}, bf16[2,256,256]{2,1,0:T(8,128)(2,1)}, u32[]{:S(2)}) copy-start(bf16[2,256,256]{2,1,0:T(8,128)(2,1)} %get-tuple-element.31) | copy-start | bytes 786436
  31.1 3.9 %copy-start.13 = (s32[24,5]{0,1:T(8,128)S(1)}, s32[24,5]{0,1:T(8,128)}, u32[]{:S(2)}) copy-start(s32[24,5]{0,1:T(8,128)} %param.21) | copy-start | bytes 1444
  34.5 14.0 %collective-permute-start.8 = (bf16[2,256,256]{2,1,0:T(8,128)(2,1)S(1)}, bf16[2,256,256]{2,1,0:T(8,128)(2,1)S(1)}, u32[]{:S(2)}, u32[]{:S(2)}) collective-permute-start(bf16[2,256,256]{2,1,0:T(8,128)(2,1)S(1)} %copy-done.17), channel_id=1, source_target_pairs={{0,4},{4,0},{8,12},{12,8},{16,20},{20,16},{24,28},{28,24},{1,5},{5... | collective-permute-start | bytes 786440 | tf_op jit(solution)/shard_map/ppermute | solution.py:26
  35.2 16.0 %collective-permute-start.9 = (bf16[2,256,256]{2,1,0:T(8,128)(2,1)}, bf16[2,256,256]{2,1,0:T(8,128)(2,1)S(1)}, u32[]{:S(2)}, u32[]{:S(2)}) collective-permute-start(bf16[2,256,256]{2,1,0:T(8,128)(2,1)} %get-tuple-element.32), channel_id=1, source_target_pairs={{0,8},{4,12},{8,0},{12,4},{16,24},{20,28},{24,16},{28,20},{1,9},{5... | collective-permute-start | bytes 786440 | tf_op jit(solution)/shard_map/ppermute | solution.py:26
  35.7 31.9 %collective-permute-start.12 = (bf16[2,256,256]{2,1,0:T(8,128)(2,1)}, bf16[2,256,256]{2,1,0:T(8,128)(2,1)S(1)}, u32[]{:S(2)}, u32[]{:S(2)}) collective-permute-start(bf16[2,256,256]{2,1,0:T(8,128)(2,1)} %get-tuple-element.35), channel_id=1, source_target_pairs={{0,4},{4,0},{8,12},{12,8},{16,20},{20,16},{24,28},{28,24},{1,5},{5... | collective-permute-start | bytes 786440 | tf_op jit(solution)/shard_map/ppermute | solution.py:26
  37.2 30.4 %collective-permute-start.13 = (bf16[2,256,256]{2,1,0:T(8,128)(2,1)}, bf16[2,256,256]{2,1,0:T(8,128)(2,1)S(1)}, u32[]{:S(2)}, u32[]{:S(2)}) collective-permute-start(bf16[2,256,256]{2,1,0:T(8,128)(2,1)} %get-tuple-element.36), channel_id=1, source_target_pairs={{0,8},{4,12},{8,0},{12,4},{16,24},{20,28},{24,16},{28,20},{1,9},{5... | collective-permute-start | bytes 786440 | tf_op jit(solution)/shard_map/ppermute | solution.py:26
  38.8 5.1 %copy-start.15 = (s32[72]{0:T(128)S(1)}, s32[72]{0:T(128)}, u32[]{:S(2)}) copy-start(s32[72]{0:T(128)} %owner_hbm.1) | copy-start | bytes 868
  38.9 24.2 %copy-start.6 = (bf16[2,256,256]{2,1,0:T(8,128)(2,1)S(1)}, bf16[2,256,256]{2,1,0:T(8,128)(2,1)}, u32[]{:S(2)}) copy-start(bf16[2,256,256]{2,1,0:T(8,128)(2,1)} %get-tuple-element.30.rest_0_) | copy-start | bytes 786436
  39.7 27.8 %copy-start.5 = (bf16[2,256,256]{2,1,0:T(8,128)(2,1)S(1)}, bf16[2,256,256]{2,1,0:T(8,128)(2,1)}, u32[]{:S(2)}) copy-start(bf16[2,256,256]{2,1,0:T(8,128)(2,1)} %get-tuple-element.34.rest_0_) | copy-start | bytes 786436
  39.7 52.6 %all-to-all-start = ((bf16[8,48,512]{2,1,0:T(8,128)(2,1)}), bf16[8,48,512]{2,1,0:T(8,128)(2,1)S(1)}, u32[]{:S(2)}, u32[]{:S(2)}) async-start(bf16[8,48,512]{2,1,0:T(8,128)(2,1)} %bitcast.15), calls=%async_computation | async-start | bytes 786432 | tf_op jit(solution)/shard_map/all_to_all | solution.py:360
  45.7 21.9 %collective-permute-start.14 = (bf16[2,256,256]{2,1,0:T(8,128)(2,1)}, bf16[2,256,256]{2,1,0:T(8,128)(2,1)S(1)}, u32[]{:S(2)}, u32[]{:S(2)}) collective-permute-start(bf16[2,256,256]{2,1,0:T(8,128)(2,1)} %get-tuple-element.37), channel_id=1, source_target_pairs={{0,12},{4,8},{8,4},{12,0},{16,28},{20,24},{24,20},{28,16},{1,13},{... | collective-permute-start | bytes 786440 | tf_op jit(solution)/shard_map/ppermute | solution.py:26
  48.4 14.7 %collective-permute-start.7 = (bf16[192,512]{1,0:T(8,128)(2,1)S(1)}, bf16[192,512]{1,0:T(8,128)(2,1)S(1)}, u32[]{:S(2)}, u32[]{:S(2)}) collective-permute-start(bf16[192,512]{1,0:T(8,128)(2,1)S(1)} %fusion.6.own_query_ref), channel_id=1, source_target_pairs={{0,16},{4,20},{8,24},{12,28},{16,0},{20,4},{24,8},{28,12},{1,17},{... | collective-permute-start | bytes 589832 | tf_op jit(solution)/shard_map/ppermute | solution.py:26
  64.1 17.0 %collective-permute-start.11 = (bf16[2,192,256]{2,1,0:T(8,128)(2,1)S(1)}, bf16[2,192,256]{2,1,0:T(8,128)(2,1)S(1)}, u32[]{:S(2)}, u32[]{:S(2)}) collective-permute-start(bf16[2,192,256]{2,1,0:T(8,128)(2,1)S(1)} %attend.2.mine_ref), channel_id=1, source_target_pairs={{0,16},{4,20},{8,24},{12,28},{16,0},{20,4},{24,8},{28,12},{1,17},{... | collective-permute-start | bytes 589832 | tf_op jit(solution)/shard_map/ppermute | solution.py:26
  68.6 15.5 %collective-permute-start.15 = (bf16[2,192,256]{2,1,0:T(8,128)(2,1)S(1)}, bf16[2,192,256]{2,1,0:T(8,128)(2,1)S(1)}, u32[]{:S(2)}, u32[]{:S(2)}) collective-permute-start(bf16[2,192,256]{2,1,0:T(8,128)(2,1)S(1)} %attend.3.mine_ref), channel_id=1, source_target_pairs={{0,16},{4,20},{8,24},{12,28},{16,0},{20,4},{24,8},{28,12},{1,17},{... | collective-permute-start | bytes 589832 | tf_op jit(solution)/shard_map/ppermute | solution.py:26
  81.1 0.7 copy-start.2
  84.1 0.7 copy-start
  84.8 5.5 %copy-start.3 = (bf16[2,192,256]{2,1,0:T(8,128)(2,1)S(1)}, bf16[2,192,256]{2,1,0:T(8,128)(2,1)}, u32[]{:S(2)}) copy-start(bf16[2,192,256]{2,1,0:T(8,128)(2,1)} %copy-done.2) | copy-start | bytes 589828
  84.8 5.6 %copy-start.1 = (bf16[2,192,256]{2,1,0:T(8,128)(2,1)S(1)}, bf16[2,192,256]{2,1,0:T(8,128)(2,1)}, u32[]{:S(2)}) copy-start(bf16[2,192,256]{2,1,0:T(8,128)(2,1)} %copy-done) | copy-start | bytes 589828
  89.4 4.7 %copy-start.16 = (bf16[192,1024]{1,0:T(8,128)(2,1)S(1)}, bf16[192,1024]{1,0:T(8,128)(2,1)}, u32[]{:S(2)}) copy-start(bf16[192,1024]{1,0:T(8,128)(2,1)} %get-tuple-element.39) | copy-start | bytes 1179652
  89.4 5.0 %copy-start.12 = (bf16[192,1024]{1,0:T(8,128)(2,1)S(1)}, bf16[192,1024]{1,0:T(8,128)(2,1)}, u32[]{:S(2)}) copy-start(bf16[192,1024]{1,0:T(8,128)(2,1)} %get-tuple-element.40) | copy-start | bytes 1179652
  89.5 4.7 %collective-permute-start.17 = (bf16[192,1024]{1,0:T(8,128)(2,1)}, bf16[192,1024]{1,0:T(8,128)(2,1)S(1)}, u32[]{:S(2)}, u32[]{:S(2)}) collective-permute-start(bf16[192,1024]{1,0:T(8,128)(2,1)} %get-tuple-element.41), channel_id=1, source_target_pairs={{0,1},{1,0},{2,3},{3,2},{4,5},{5,4},{6,7},{7,6},{8,9},{9,8},{10,11... | collective-permute-start | bytes 1179656 | tf_op jit(solution)/shard_map/ppermute | solution.py:26
  90.3 14.2 %collective-permute-start.26 = (bf16[2,192,256]{2,1,0:T(8,128)(2,1)S(1)}, bf16[2,192,256]{2,1,0:T(8,128)(2,1)S(1)}, u32[]{:S(2)}, u32[]{:S(2)}) collective-permute-start(bf16[2,192,256]{2,1,0:T(8,128)(2,1)S(1)} %copy-done.3), channel_id=1, source_target_pairs={{0,8},{4,12},{8,0},{12,4},{16,24},{20,28},{24,16},{28,20},{1,9},{5... | collective-permute-start | bytes 589832 | tf_op jit(solution)/shard_map/ppermute | solution.py:26
  90.4 15.7 %collective-permute-start.23 = (bf16[2,192,256]{2,1,0:T(8,128)(2,1)S(1)}, bf16[2,192,256]{2,1,0:T(8,128)(2,1)S(1)}, u32[]{:S(2)}, u32[]{:S(2)}) collective-permute-start(bf16[2,192,256]{2,1,0:T(8,128)(2,1)S(1)} %copy-done.1), channel_id=1, source_target_pairs={{0,8},{4,12},{8,0},{12,4},{16,24},{20,28},{24,16},{28,20},{1,9},{5... | collective-permute-start | bytes 589832 | tf_op jit(solution)/shard_map/ppermute | solution.py:26
  92.4 2.2 %collective-permute-start.19 = (bf16[8,48,512]{2,1,0:T(8,128)(2,1)S(1)}, bf16[8,48,512]{2,1,0:T(8,128)(2,1)S(1)}, u32[]{:S(2)}, u32[]{:S(2)}) collective-permute-start(bf16[8,48,512]{2,1,0:T(8,128)(2,1)S(1)} %all-to-all-done), channel_id=1, source_target_pairs={{0,1},{1,0},{2,3},{3,2},{4,5},{5,4},{6,7},{7,6},{8,9},{9,8},{10,11... | collective-permute-start | bytes 1179656 | tf_op jit(solution)/shard_map/ppermute | solution.py:26
  92.4 12.0 %collective-permute-start.20 = (bf16[8,48,512]{2,1,0:T(8,128)(2,1)S(1)}, bf16[8,48,512]{2,1,0:T(8,128)(2,1)S(1)}, u32[]{:S(2)}, u32[]{:S(2)}) collective-permute-start(bf16[8,48,512]{2,1,0:T(8,128)(2,1)S(1)} %all-to-all-done), channel_id=1, source_target_pairs={{0,2},{1,3},{2,0},{3,1},{4,6},{5,7},{6,4},{7,5},{8,10},{9,11},{10,... | collective-permute-start | bytes 1179656 | tf_op jit(solution)/shard_map/ppermute | solution.py:26
  94.1 19.7 %copy-start.11 = (bf16[192,1024]{1,0:T(8,128)(2,1)S(1)}, bf16[192,1024]{1,0:T(8,128)(2,1)}, u32[]{:S(2)}) copy-start(bf16[192,1024]{1,0:T(8,128)(2,1)} %get-tuple-element.38) | copy-start | bytes 1179652
  94.2 12.4 %collective-permute-start.16 = (bf16[192,1024]{1,0:T(8,128)(2,1)S(1)}, bf16[192,1024]{1,0:T(8,128)(2,1)S(1)}, u32[]{:S(2)}, u32[]{:S(2)}) collective-permute-start(bf16[192,1024]{1,0:T(8,128)(2,1)S(1)} %copy-done.16), channel_id=1, source_target_pairs={{0,1},{1,0},{2,3},{3,2},{4,5},{5,4},{6,7},{7,6},{8,9},{9,8},{10,11... | collective-permute-start | bytes 1179656 | tf_op jit(solution)/shard_map/ppermute | solution.py:26
  94.6 17.7 %collective-permute-start.18 = (bf16[192,1024]{1,0:T(8,128)(2,1)S(1)}, bf16[192,1024]{1,0:T(8,128)(2,1)S(1)}, u32[]{:S(2)}, u32[]{:S(2)}) collective-permute-start(bf16[192,1024]{1,0:T(8,128)(2,1)S(1)} %add_convert_fusion.1), channel_id=1, source_target_pairs={{0,2},{1,3},{2,0},{3,1},{4,6},{5,7},{6,4},{7,5},{8,10},{9,11},{10,... | collective-permute-start | bytes 1179656 | tf_op jit(solution)/shard_map/ppermute | solution.py:26
  104.4 10.5 %collective-permute-start.21 = (bf16[8,48,512]{2,1,0:T(8,128)(2,1)S(1)}, bf16[8,48,512]{2,1,0:T(8,128)(2,1)S(1)}, u32[]{:S(2)}, u32[]{:S(2)}) collective-permute-start(bf16[8,48,512]{2,1,0:T(8,128)(2,1)S(1)} %collective-permute-done.20), channel_id=1, source_target_pairs={{0,1},{1,0},{2,3},{3,2},{4,5},{5,4},{6,7},{7,6},{8,9},{9,8},{10,11... | collective-permute-start | bytes 1179656 | tf_op jit(solution)/shard_map/ppermute | solution.py:26
  104.5 16.3 %copy-start.10 = (s32[2]{0:T(128)S(1)}, s32[2]{0:T(128)}, u32[]{:S(2)}) copy-start(s32[2]{0:T(128)} %copy-done.9) | copy-start | bytes 28
  104.5 10.4 %collective-permute-start.25 = (bf16[2,192,256]{2,1,0:T(8,128)(2,1)S(1)}, bf16[2,192,256]{2,1,0:T(8,128)(2,1)S(1)}, u32[]{:S(2)}, u32[]{:S(2)}) collective-permute-start(bf16[2,192,256]{2,1,0:T(8,128)(2,1)S(1)} %copy-done.3), channel_id=1, source_target_pairs={{0,4},{4,0},{8,12},{12,8},{16,20},{20,16},{24,28},{28,24},{1,5},{5... | collective-permute-start | bytes 589832 | tf_op jit(solution)/shard_map/ppermute | solution.py:26
  106.0 15.9 %collective-permute-start.22 = (bf16[2,192,256]{2,1,0:T(8,128)(2,1)S(1)}, bf16[2,192,256]{2,1,0:T(8,128)(2,1)S(1)}, u32[]{:S(2)}, u32[]{:S(2)}) collective-permute-start(bf16[2,192,256]{2,1,0:T(8,128)(2,1)S(1)} %copy-done.1), channel_id=1, source_target_pairs={{0,4},{4,0},{8,12},{12,8},{16,20},{20,16},{24,28},{28,24},{1,5},{5... | collective-permute-start | bytes 589832 | tf_op jit(solution)/shard_map/ppermute | solution.py:26
  106.6 14.2 %collective-permute-start.27 = (bf16[2,192,256]{2,1,0:T(8,128)(2,1)S(1)}, bf16[2,192,256]{2,1,0:T(8,128)(2,1)S(1)}, u32[]{:S(2)}, u32[]{:S(2)}) collective-permute-start(bf16[2,192,256]{2,1,0:T(8,128)(2,1)S(1)} %collective-permute-done.26.rest_2_), channel_id=1, source_target_pairs={{0,4},{4,0},{8,12},{12,8},{16,20},{20,16},{24,28},{28,24},{1,5},{5... | collective-permute-start | bytes 589832 | tf_op jit(solution)/shard_map/ppermute | solution.py:26
  112.3 12.2 %collective-permute-start.24 = (bf16[2,192,256]{2,1,0:T(8,128)(2,1)S(1)}, bf16[2,192,256]{2,1,0:T(8,128)(2,1)S(1)}, u32[]{:S(2)}, u32[]{:S(2)}) collective-permute-start(bf16[2,192,256]{2,1,0:T(8,128)(2,1)S(1)} %collective-permute-done.23.rest_2_), channel_id=1, source_target_pairs={{0,4},{4,0},{8,12},{12,8},{16,20},{20,16},{24,28},{28,24},{1,5},{5... | collective-permute-start | bytes 589832 | tf_op jit(solution)/shard_map/ppermute | solution.py:26
